TPU v7x, 512 devices: a whole 4x8x8 slice. The times are simulated.
512 devices in a mesh: slab: 8 (over z), tile: 64 (over x, y, core).
Axes of the slice: x: 4, y: 8, z: 8, core: 2. Of those that a mesh axis runs over, the one named last changes fastest.
Arguments:
- voxel_grid: float32 [4, 128, 512, 256], P(None, 'slab', 'tile'), may hold values from -4 to 4
- first_moment: float32 [4, 128, 512, 256], P(None, 'slab', 'tile'), may hold values from -0.75 to 0.75
- second_moment: float32 [4, 128, 512, 256], P(None, 'slab', 'tile'), may hold values from 0.01 to 0.5
- pixel_index: int32 [262144], P('tile'), may hold values from 0 to 2047
- start_slab: int32 [262144], P('tile'), may hold values from 0 to 3
- ray_count: int32 [262144], P('tile'), may hold values from 32 to 80
- target: float32 [3, 262144], P(None, 'tile'), may hold values from 0 to 1
Outputs:
- new_grid: float32 [4, 128, 512, 256], P(None, 'slab', 'tile')
- new_first: float32 [4, 128, 512, 256], P(None, 'slab', 'tile')
- new_second: float32 [4, 128, 512, 256], P(None, 'slab', 'tile')
All inputs are finite; a program needn't handle non-finite values.
Results may differ from a plain program's by a relative error of at most 0.0003.
Values sent between devices are 32-bit elements; how exact they have to be, the bound alone decides.
A program may use at most 128 MiB of HBM per device.

v0:
```python
import functools
import math

import jax
import jax.numpy as jnp
from jax import lax
from jax.sharding import Mesh
from jax.sharding import PartitionSpec as P

STEP = 20
TILE = ("tile_0", "tile_1", "tile_2")
SLAB_TILE = ("slab", "tile_0", "tile_1", "tile_2")


RENDER_WEIGHT = 1000.0
TV_WEIGHT = 0.05
BACKGROUND = 1.0
STEP_SPAN = 4.0
CLIP_RMS = 0.25
LEARN_RATE = 0.02
BETA_ONE = 0.9
BETA_TWO = 0.99
EPSILON = 1e-08
BLOCK_LIMIT = 1024


def with_halo(array, sides, width):
    edges = {}
    for axis, dim in sides:
        size, length = (lax.axis_size(axis), array.shape[dim])
        up = [(i, (i + 1) % size) for i in range(size - 1)]
        last = lax.slice_in_dim(array, length - width, length, axis=dim)
        initial = lax.slice_in_dim(array, 0, width, axis=dim)
        edges[dim] = (
            lax.ppermute(last, axis, up),
            lax.ppermute(initial, axis, [(b, a) for a, b in up]),
        )
    done = []
    for _, dim in sides:
        low, high = edges[dim]
        around = [(width, width) if d in done else (0, 0) for d in range(array.ndim)]
        array = jnp.concatenate([jnp.pad(low, around), array, jnp.pad(high, around)], axis=dim)
        done.append(dim)
    return array


def copy_for_each(array, axis):
    length = lax.axis_size(axis)
    return lax.all_to_all(
        jnp.broadcast_to(array[None], (length, *array.shape)), axis, 0, 0, tiled=True
    )


def all_in_one(array, axis):
    leaves = jax.tree.leaves(array)
    order = sorted(range(len(leaves)), key=lambda k: -leaves[k].size)
    width = (1, *leaves[order[0]].shape)[-1]
    lines = [
        jnp.pad(leaves[k].reshape(-1), (0, -leaves[k].size % width)).reshape(-1, width)
        for k in order
    ]
    both, at, found = (copy_for_each(jnp.concatenate(lines), axis), 0, {})
    for k, line in zip(order, lines):
        piece = both[:, at : at + len(line)].reshape(len(both), -1)
        found[k] = piece[:, : leaves[k].size].reshape(-1, *leaves[k].shape)
        at += len(line)
    numbers = iter(range(len(leaves)))
    return jax.tree.map(lambda _: found[next(numbers)], array)


def combined_pairwise(pieces, combine):
    while len(jax.tree.leaves(pieces)[0]) > 1:
        pieces = jax.vmap(combine)(
            *(jax.tree.map(lambda part: part[side::2], pieces) for side in (0, 1))
        )
    return jax.tree.map(lambda part: part[0], pieces)


def prefix(array, axis, combine, identity, reverse):
    length, place = (lax.axis_size(axis), lax.axis_index(axis))
    passed = jnp.arange(length) > place if reverse else jnp.arange(length) < place

    def kept(part, zero, own):
        part = jnp.where(
            passed.reshape(-1, *(1 for _ in own.shape)), part, jnp.asarray(zero, own.dtype)
        )
        return part[::-1] if reverse else part

    pieces = all_in_one(array, axis)
    return combined_pairwise(jax.tree.map(kept, pieces, identity, array), combine)


def one_axis_at_a_time(array, axes):
    return functools.reduce(lax.psum, axes, array)


def front_join(earlier, later):
    return (earlier[0] + earlier[1][None] * later[0], earlier[1] * later[1])


def back_join(earlier, later):
    return (later[0] + later[1][None] * earlier[0], later[1] * earlier[1])


def per_device(voxel_grid, first_moment, second_moment, pixel_index, start_slab, ray_count, target):
    slab_count = lax.axis_size("slab")
    tile_count = lax.axis_size(TILE)
    slab_pos = lax.axis_index("slab")
    tile_pos = lax.axis_index(TILE)
    channels, slab_depth, rows_x, rows_y = voxel_grid.shape
    total_depth = slab_depth * slab_count
    total_x = rows_x * tile_count
    pixel_total = rows_x * rows_y
    ray_total = pixel_index.shape[0]
    ray_block = math.gcd(ray_total, BLOCK_LIMIT)
    block_count = ray_total // ray_block
    padded = with_halo(voxel_grid, (("slab", 1), (TILE, 2)), 1)
    depth_pos = slab_pos * slab_depth + jnp.arange(slab_depth, dtype=jnp.int32)
    first_cell = start_slab[None, :] * (total_depth // slab_count)
    inside = (depth_pos[:, None] >= first_cell) & (
        depth_pos[:, None] < first_cell + ray_count[None, :]
    )
    pixel_blocks = pixel_index.reshape(block_count, ray_block)
    pixel_ids = jnp.arange(pixel_total, dtype=jnp.int32)
    depth_ids = jnp.arange(slab_depth, dtype=jnp.int32)
    lower = (depth_ids[:, None] >= depth_ids[None, :]).astype(jnp.float32)

    def march_slab(local_grid):
        flat = local_grid.reshape(channels * slab_depth, pixel_total)

        def pick_block(block_pixels):
            selector = (pixel_ids[:, None] == block_pixels[None, :]).astype(jnp.float32)
            return jnp.dot(
                flat, selector, precision=lax.Precision.HIGHEST, preferred_element_type=jnp.float32
            )

        picked = lax.map(pick_block, pixel_blocks)
        samples = picked.transpose(1, 0, 2).reshape(channels, slab_depth, ray_total)
        optical = jnp.where(inside, jax.nn.softplus(samples[0]) * (STEP_SPAN / total_depth), 0.0)
        running = jnp.dot(
            lower, optical, precision=lax.Precision.HIGHEST, preferred_element_type=jnp.float32
        )
        weights = jnp.exp(-(running - optical)) * (1.0 - jnp.exp(-optical))
        colors = jax.nn.sigmoid(samples[1:4])
        return (jnp.sum(weights[None] * colors, axis=1), jnp.exp(-running[-1]))

    (part_color, part_trans), pullback = jax.vjp(march_slab, voxel_grid)
    empty = (jnp.zeros_like(part_color), jnp.ones_like(part_trans))
    front_color, front_trans = prefix((part_color, part_trans), "slab", front_join, empty, False)
    back_color, back_trans = prefix((part_color, part_trans), "slab", back_join, empty, True)
    beyond = back_color + back_trans[None] * BACKGROUND
    rendered = front_color + front_trans[None] * (part_color + part_trans[None] * beyond)
    residual = RENDER_WEIGHT * (rendered - target)
    color_cot = front_trans[None] * residual
    trans_cot = front_trans * jnp.sum(residual * beyond, axis=0)
    render_grad = pullback((color_cot, trans_cot))[0]
    depth_view = depth_pos.reshape(1, slab_depth, 1, 1)
    x_view = (tile_pos * rows_x + jnp.arange(rows_x, dtype=jnp.int32)).reshape(1, 1, rows_x, 1)
    smooth = jnp.where(depth_view > 0, voxel_grid - padded[:, :-2, 1:-1, :], 0.0)
    smooth = smooth + jnp.where(
        depth_view < total_depth - 1, voxel_grid - padded[:, 2:, 1:-1, :], 0.0
    )
    smooth = smooth + jnp.where(x_view > 0, voxel_grid - padded[:, 1:-1, :-2, :], 0.0)
    smooth = smooth + jnp.where(x_view < total_x - 1, voxel_grid - padded[:, 1:-1, 2:, :], 0.0)
    step_y = jnp.diff(voxel_grid, axis=3)
    smooth = (
        smooth
        + jnp.pad(-step_y, ((0, 0), (0, 0), (0, 0), (0, 1)))
        + jnp.pad(step_y, ((0, 0), (0, 0), (0, 0), (1, 0)))
    )
    gradient = render_grad + 2.0 * TV_WEIGHT * smooth
    square_sum = one_axis_at_a_time(jnp.sum(gradient * gradient), SLAB_TILE)
    norm_value = jnp.sqrt(square_sum)
    limit = CLIP_RMS * math.sqrt(4.0 * total_depth * total_x * rows_y)
    clipped = gradient * (limit / jnp.maximum(norm_value, limit))
    new_first = BETA_ONE * first_moment + (1.0 - BETA_ONE) * clipped
    new_second = BETA_TWO * second_moment + (1.0 - BETA_TWO) * clipped * clipped
    first_hat = new_first / (1.0 - BETA_ONE**STEP)
    second_hat = new_second / (1.0 - BETA_TWO**STEP)
    new_grid = voxel_grid - LEARN_RATE * first_hat / (jnp.sqrt(second_hat) + EPSILON)
    return (new_grid, new_first, new_second)


def solution(mesh):
    torus = Mesh(
        mesh.devices.reshape(mesh.shape["slab"], 4, 8, 2), ("slab", "tile_0", "tile_1", "tile_2")
    )
    in_specs = (
        P(None, "slab", TILE, None),
        P(None, "slab", TILE, None),
        P(None, "slab", TILE, None),
        P(TILE),
        P(TILE),
        P(TILE),
        P(None, TILE),
    )
    out_specs = (
        P(None, "slab", TILE, None),
        P(None, "slab", TILE, None),
        P(None, "slab", TILE, None),
    )
    return jax.shard_map(
        per_device, mesh=torus, in_specs=in_specs, out_specs=out_specs, check_vma=False
    )
```

profile of v0, /device:TPU:1, one launch (start us, length us, event | category | flops | bytes accessed | tf_op | source)
XLA Modules:
  0.0 170.5 jit_solution(15467916179743026373)
XLA Ops:
  0.7 1.2 copy.26
  1.9 0.7 reshape.162
  2.6 30.4 %while.29 = (s32[]{:T(128)}, f32[4,64,1024]{2,1,0:T(8,128)S(1)}, f32[4,2048,1024]{2,1,0:T(8,128)}, s32[4,1024]{1,0:T(4,128)S(1)}, f32[64,2048]{1,0:T(8,128)S(1)}, /*index=5*/s32[]{:T(128)}) while((s32[]{:T(128)}, f32[4,64,1024]{2,1,0:T(8,128)S(1)}, f32[4,2048,1024]{2,1,0:T(8,128)}, s32[4,1024]{1,0:T(4,128)S(1)}, ...), condition=%wide.region_1.2_spmd.clone.clone, body=%wide.region_0.1_spmd.clone.clone.sunk | while | flops 1616904192 | bytes 9192013 | solution.py:137
  2.6 3.1 %fusion.78 = f32[4,64,1024]{2,1,0:T(8,128)S(1)} fusion(f32[4,64,1024]{2,1,0:T(8,128)S(1)} %get-tuple-element.285, s32[]{:T(128)} %get-tuple-element.284, f32[64,2048]{1,0:T(8,128)S(1)} %get-tuple-element.294, s32[1024]{0:T(1024)S(1)} %bitcast.78), kind=kOutput, calls=%fused_computation.7.clone.1 | convolution fusion | flops 1612709888 | bytes 790532 | tf_op jit(solution)/shard_map/jvp()/while/body/eval_jaxpr/dot_general | solution.py:133
  5.8 4.5 %convert_dynamic-update-slice_fusion.2 = f32[4,2048,1024]{2,1,0:T(8,128)} fusion(f32[4,2048,1024]{2,1,0:T(8,128)} %get-tuple-element.286, s32[]{:T(128)} %get-tuple-element.284, s32[1024]{0:T(1024)S(1)} %bitcast.79), kind=kLoop, calls=%fused_computation.3.clone.1 | loop fusion | flops 4194304 | bytes 8393216 | tf_op jit(solution)/shard_map/jvp()/while/body/jit(dynamic_update_index_in_dim)/dynamic_update_slice | solution.py:137
  10.2 3.1 %fusion.78 = f32[4,64,1024]{2,1,0:T(8,128)S(1)} fusion(f32[4,64,1024]{2,1,0:T(8,128)S(1)} %get-tuple-element.285, s32[]{:T(128)} %get-tuple-element.284, f32[64,2048]{1,0:T(8,128)S(1)} %get-tuple-element.294, s32[1024]{0:T(1024)S(1)} %bitcast.78), kind=kOutput, calls=%fused_computation.7.clone.1 | convolution fusion | flops 1612709888 | bytes 790532 | tf_op jit(solution)/shard_map/jvp()/while/body/eval_jaxpr/dot_general | solution.py:133
  13.4 4.5 %convert_dynamic-update-slice_fusion.2 = f32[4,2048,1024]{2,1,0:T(8,128)} fusion(f32[4,2048,1024]{2,1,0:T(8,128)} %get-tuple-element.286, s32[]{:T(128)} %get-tuple-element.284, s32[1024]{0:T(1024)S(1)} %bitcast.79), kind=kLoop, calls=%fused_computation.3.clone.1 | loop fusion | flops 4194304 | bytes 8393216 | tf_op jit(solution)/shard_map/jvp()/while/body/jit(dynamic_update_index_in_dim)/dynamic_update_slice | solution.py:137
  17.8 3.1 %fusion.78 = f32[4,64,1024]{2,1,0:T(8,128)S(1)} fusion(f32[4,64,1024]{2,1,0:T(8,128)S(1)} %get-tuple-element.285, s32[]{:T(128)} %get-tuple-element.284, f32[64,2048]{1,0:T(8,128)S(1)} %get-tuple-element.294, s32[1024]{0:T(1024)S(1)} %bitcast.78), kind=kOutput, calls=%fused_computation.7.clone.1 | convolution fusion | flops 1612709888 | bytes 790532 | tf_op jit(solution)/shard_map/jvp()/while/body/eval_jaxpr/dot_general | solution.py:133
  21.0 4.5 %convert_dynamic-update-slice_fusion.2 = f32[4,2048,1024]{2,1,0:T(8,128)} fusion(f32[4,2048,1024]{2,1,0:T(8,128)} %get-tuple-element.286, s32[]{:T(128)} %get-tuple-element.284, s32[1024]{0:T(1024)S(1)} %bitcast.79), kind=kLoop, calls=%fused_computation.3.clone.1 | loop fusion | flops 4194304 | bytes 8393216 | tf_op jit(solution)/shard_map/jvp()/while/body/jit(dynamic_update_index_in_dim)/dynamic_update_slice | solution.py:137
  25.4 3.1 %fusion.78 = f32[4,64,1024]{2,1,0:T(8,128)S(1)} fusion(f32[4,64,1024]{2,1,0:T(8,128)S(1)} %get-tuple-element.285, s32[]{:T(128)} %get-tuple-element.284, f32[64,2048]{1,0:T(8,128)S(1)} %get-tuple-element.294, s32[1024]{0:T(1024)S(1)} %bitcast.78), kind=kOutput, calls=%fused_computation.7.clone.1 | convolution fusion | flops 1612709888 | bytes 790532 | tf_op jit(solution)/shard_map/jvp()/while/body/eval_jaxpr/dot_general | solution.py:133
  28.6 4.5 %convert_dynamic-update-slice_fusion.2 = f32[4,2048,1024]{2,1,0:T(8,128)} fusion(f32[4,2048,1024]{2,1,0:T(8,128)} %get-tuple-element.286, s32[]{:T(128)} %get-tuple-element.284, s32[1024]{0:T(1024)S(1)} %bitcast.79), kind=kLoop, calls=%fused_computation.3.clone.1 | loop fusion | flops 4194304 | bytes 8393216 | tf_op jit(solution)/shard_map/jvp()/while/body/jit(dynamic_update_index_in_dim)/dynamic_update_slice | solution.py:137
  33.0 0.2 fusion.22
  33.3 0.5 copy.21
  33.8 0.5 div.21
  34.4 0.6 subtract_multiply_fusion.1
  35.1 0.7 copy-done.10
  35.8 0.2 multiply_reduce_fusion.1
  36.0 0.9 broadcast_in_dim.128
  36.9 10.9 %all-to-all-start = ((f32[8,4,4096]{2,1,0:T(4,128)}), f32[8,4,4096]{2,1,0:T(4,128)S(1)}, u32[]{:S(2)}, u32[]{:S(2)}) async-start(f32[8,4,4096]{2,1,0:T(4,128)} %broadcast_in_dim.128), calls=%async_computation | async-start | bytes 1048576 | tf_op jit(solution)/shard_map/all_to_all | solution.py:49
  47.7 3.4 %collective-permute-start = (f32[4,1,8,256]{3,2,1,0:T(8,128)S(1)}, f32[4,1,8,256]{3,2,1,0:T(8,128)S(1)}, u32[]{:S(2)}, u32[]{:S(2)}) collective-permute-start(f32[4,1,8,256]{3,2,1,0:T(8,128)S(1)} %get-tuple-element.205), channel_id=1, source_target_pairs={{0,64},{64,128},{128,192},{192,256},{256,320},{320,384},{384,448},... | collective-permute-start | bytes 98312 | tf_op jit(solution)/shard_map/ppermute | solution.py:35
  51.1 1.3 collective-permute-start.1
  52.4 0.7 fusion.67
  53.2 4.6 %collective-permute-start.2 = (f32[4,16,1,256]{3,2,1,0:T(1,128)}, f32[4,16,1,256]{3,2,1,0:T(1,128)}, u32[]{:S(2)}, u32[]{:S(2)}) collective-permute-start(f32[4,16,1,256]{3,2,1,0:T(1,128)} %get-tuple-element.202), channel_id=1, source_target_pairs={{0,1},{1,2},{2,3},{3,4},{4,5},{5,6},{6,7},{7,8},{8,9},{9,10},{10,1... | collective-permute-start | bytes 196616 | tf_op jit(solution)/shard_map/ppermute | solution.py:35
  57.8 2.1 %collective-permute-start.3 = (f32[4,16,1,256]{3,2,1,0:T(1,128)}, f32[4,16,1,256]{3,2,1,0:T(1,128)}, u32[]{:S(2)}, u32[]{:S(2)}) collective-permute-start(f32[4,16,1,256]{3,2,1,0:T(1,128)} %get-tuple-element.203), channel_id=1, source_target_pairs={{1,0},{2,1},{3,2},{4,3},{5,4},{6,5},{7,6},{8,7},{9,8},{10,9},{11,1... | collective-permute-start | bytes 196616 | tf_op jit(solution)/shard_map/ppermute | solution.py:36
  59.9 0.5 broadcast_compare_fusion
  60.5 1.2 fusion.64
  61.6 0.6 fusion.58
  62.2 0.6 constant_dynamic-update-slice_fusion.2
  62.8 0.8 constant_dynamic-update-slice_fusion.1
  63.7 0.6 constant_dynamic-update-slice_fusion
  64.3 0.9 all-to-all-done
  65.2 0.1 slice.194
  65.3 0.1 fusion.47
  65.4 0.1 slice.153
  65.6 0.1 slice.156
  65.7 0.1 slice.166
  65.8 0.1 slice.171
  65.9 0.8 slice.167
  66.7 0.8 slice.172
  67.5 0.1 slice.173
  67.7 0.1 slice.176
  67.8 0.1 slice.157
  67.9 0.1 slice.160
  68.1 1.0 slice_select_fusion.1
  69.1 0.1 multiply_add_fusion.2
  69.2 0.1 fusion.66
  69.3 0.1 multiply_add_fusion.1
  69.6 0.1 broadcast_multiply_fusion
  69.7 0.2 fusion.19
  70.1 0.9 fusion.18
  71.0 0.7 reshape.165
  71.7 0.6 copy.34
  72.4 41.8 %while.30 = (s32[]{:T(128)}, f32[64,2048]{1,0:T(8,128)S(1)}, f32[4,64,1024]{2,1,0:T(8,128)S(1)}, f32[4,2048,1024]{2,1,0:T(8,128)}, s32[]{:T(128)}, /*index=5*/s32[]{:T(128)}, s32[]{:T(128)}) while((s32[]{:T(128)}, f32[64,2048]{1,0:T(8,128)S(1)}, f32[4,64,1024]{2,1,0:T(8,128)S(1)}, f32[4,2048,1024]{2,1,0:T(8,128)}, s32[]{:T(128)}, ...), condition=%wide.region_6.7_spmd.clone, body=%wide.region_5.6_spmd.clone.sunk | while | flops 1610874880 | bytes 9700962 | solution.py:137
  72.4 10.5 %fusion.81 = f32[64,2048]{1,0:T(8,128)S(1)} fusion(f32[4,2048,1024]{2,1,0:T(8,128)} %get-tuple-element.313, s32[]{:T(128)S(6)} %sub.127, f32[64,2048]{1,0:T(8,128)S(1)} %get-tuple-element.304, f32[4,64,1024]{2,1,0:T(8,128)S(1)} %get-tuple-element.312, pred[]{:T(512)S(6)} %compare.20), kind=kOutput, calls=%fused_computation.12.clone.1 | convolution fusion | flops 1610874880 | bytes 9700864 | tf_op jit(solution)/shard_map/transpose(jvp())/while/body/eval_jaxpr/dot_general | solution.py:133
  82.9 10.4 %fusion.81 = f32[64,2048]{1,0:T(8,128)S(1)} fusion(f32[4,2048,1024]{2,1,0:T(8,128)} %get-tuple-element.313, s32[]{:T(128)S(6)} %sub.127, f32[64,2048]{1,0:T(8,128)S(1)} %get-tuple-element.304, f32[4,64,1024]{2,1,0:T(8,128)S(1)} %get-tuple-element.312, pred[]{:T(512)S(6)} %compare.20), kind=kOutput, calls=%fused_computation.12.clone.1 | convolution fusion | flops 1610874880 | bytes 9700864 | tf_op jit(solution)/shard_map/transpose(jvp())/while/body/eval_jaxpr/dot_general | solution.py:133
  93.3 10.4 %fusion.81 = f32[64,2048]{1,0:T(8,128)S(1)} fusion(f32[4,2048,1024]{2,1,0:T(8,128)} %get-tuple-element.313, s32[]{:T(128)S(6)} %sub.127, f32[64,2048]{1,0:T(8,128)S(1)} %get-tuple-element.304, f32[4,64,1024]{2,1,0:T(8,128)S(1)} %get-tuple-element.312, pred[]{:T(512)S(6)} %compare.20), kind=kOutput, calls=%fused_computation.12.clone.1 | convolution fusion | flops 1610874880 | bytes 9700864 | tf_op jit(solution)/shard_map/transpose(jvp())/while/body/eval_jaxpr/dot_general | solution.py:133
  103.8 10.4 %fusion.81 = f32[64,2048]{1,0:T(8,128)S(1)} fusion(f32[4,2048,1024]{2,1,0:T(8,128)} %get-tuple-element.313, s32[]{:T(128)S(6)} %sub.127, f32[64,2048]{1,0:T(8,128)S(1)} %get-tuple-element.304, f32[4,64,1024]{2,1,0:T(8,128)S(1)} %get-tuple-element.312, pred[]{:T(512)S(6)} %compare.20), kind=kOutput, calls=%fused_computation.12.clone.1 | convolution fusion | flops 1610874880 | bytes 9700864 | tf_op jit(solution)/shard_map/transpose(jvp())/while/body/eval_jaxpr/dot_general | solution.py:133
  114.2 0.2 copy.27
  114.4 2.4 %multiply_reduce_fusion.2 = (f32[]{:T(128)}, f32[4,16,8,256]{3,2,1,0:T(8,128)S(1)}) fusion(f32[4,16,8,255]{3,2,1,0:T(8,128)S(1)} %copy-done.2, f32[4,16,8,255]{3,2,1,0:T(8,128)S(1)} %copy-done.1, f32[4,16,8,256]{3,2,1,0:T(8,128)S(1)} %copy-done, f32[4,16,1,256]{3,2,1,0:T(1,128)} %collective-permute-done.3, ...), kind=kLoop, calls=%fused_computation.61 | loop fusion | flops 3538943 | bytes 3403828 | tf_op jit(solution)/shard_map/reduce_sum | solution.py:172
  116.8 14.0 %psum.28 = f32[]{:T(128)} all-reduce(f32[]{:T(128)} %get-tuple-element.190), channel_id=1, replica_groups=mesh['slab'=8,'tile_0'=4,'tile_1'=8,'tile_2'=2] {'slab'}, use_global_device_ids=true, to_apply=%region_8.9 | all-reduce | flops 1 | bytes 8 | tf_op jit(solution)/shard_map/psum | solution.py:94
  130.8 9.1 %psum.29 = f32[]{:T(128)} all-reduce(f32[]{:T(128)} %psum.28), channel_id=1, replica_groups=mesh['slab'=8,'tile_0'=4,'tile_1'=8,'tile_2'=2] {'tile_0'}, use_global_device_ids=true, to_apply=%region_9.10 | all-reduce | flops 1 | bytes 8 | tf_op jit(solution)/shard_map/psum | solution.py:94
  139.9 14.2 %psum.30 = f32[]{:T(128)} all-reduce(f32[]{:T(128)} %psum.29), channel_id=1, replica_groups=mesh['slab'=8,'tile_0'=4,'tile_1'=8,'tile_2'=2] {'tile_1'}, use_global_device_ids=true, to_apply=%region_10.11 | all-reduce | flops 1 | bytes 8 | tf_op jit(solution)/shard_map/psum | solution.py:94
  154.1 13.1 %psum.31 = f32[]{:T(128)} all-reduce(f32[]{:T(128)} %psum.30), channel_id=1, replica_groups=mesh['slab'=8,'tile_0'=4,'tile_1'=8,'tile_2'=2] {'tile_2'}, use_global_device_ids=true, to_apply=%region_11.12 | all-reduce | flops 1 | bytes 8 | tf_op jit(solution)/shard_map/psum | solution.py:94
  167.9 2.5 %divide_subtract_fusion = (f32[4,16,8,256]{3,2,1,0:T(8,128)}, f32[4,16,8,256]{3,2,1,0:T(8,128)}, f32[4,16,8,256]{3,2,1,0:T(8,128)}) fusion(f32[4,16,8,256]{3,2,1,0:T(8,128)S(1)} %copy-done, f32[4,16,8,256]{3,2,1,0:T(8,128)S(1)} %get-tuple-element.191, f32[]{:T(128)S(6)} %div.22, f32[4,16,8,256]{3,2,1,0:T(8,128)} %param.12, f32[4,16,8,256]{3,2,1,0:T(8,128)} %param.13), kind=kLoop, calls=%fused_computation.59 | loop fusion | flops 1703936 | bytes 3670020 | tf_op jit(solution)/shard_map/sub | solution.py:180
  (70 shorter events, 0.7 us)
Async XLA Ops:
  2.6 31.8 %copy-start.4 = (s32[4096]{0:T(1024)S(1)}, s32[4096]{0:T(1024)}, u32[]{:S(2)}) copy-start(s32[4096]{0:T(1024)} %param.15) | copy-start | bytes 49156
  2.6 31.8 %copy-start.5 = (s32[4096]{0:T(1024)S(1)}, s32[4096]{0:T(1024)}, u32[]{:S(2)}) copy-start(s32[4096]{0:T(1024)} %param.16) | copy-start | bytes 49156
  33.0 14.7 %copy-start = (f32[4,16,8,256]{3,2,1,0:T(8,128)S(1)}, f32[4,16,8,256]{3,2,1,0:T(8,128)}, u32[]{:S(2)}) copy-start(f32[4,16,8,256]{3,2,1,0:T(8,128)} %param.11) | copy-start | bytes 1572868
  33.3 17.8 %copy-start.18 = (s32[16]{0:T(128)}, s32[16]{0:T(128)S(1)}, u32[]{:S(2)}) copy-start(s32[16]{0:T(128)S(1)} %iota_add_fusion.1) | copy-start | bytes 196
  34.4 35.2 %copy-start.3 = (f32[3,4096]{1,0:T(4,128)S(1)}, f32[3,4096]{1,0:T(4,128)}, u32[]{:S(2)}) copy-start(f32[3,4096]{1,0:T(4,128)} %param.17) | copy-start | bytes 147460
  34.4 13.3 %copy-start.6 = (s32[4096]{0:T(1024)}, s32[4096]{0:T(1024)S(1)}, u32[]{:S(2)}) copy-start(s32[4096]{0:T(1024)S(1)} %get-tuple-element.212) | copy-start | bytes 49156
  34.4 16.7 %copy-start.8 = (s32[4096]{0:T(1024)}, s32[4096]{0:T(1024)S(1)}, u32[]{:S(2)}) copy-start(s32[4096]{0:T(1024)S(1)} %get-tuple-element.213) | copy-start | bytes 49156
  35.1 0.7 copy-start.10
  36.9 28.3 %all-to-all-start = ((f32[8,4,4096]{2,1,0:T(4,128)}), f32[8,4,4096]{2,1,0:T(4,128)S(1)}, u32[]{:S(2)}, u32[]{:S(2)}) async-start(f32[8,4,4096]{2,1,0:T(4,128)} %broadcast_in_dim.128), calls=%async_computation | async-start | bytes 1048576 | tf_op jit(solution)/shard_map/all_to_all | solution.py:49
  47.7 14.5 %collective-permute-start = (f32[4,1,8,256]{3,2,1,0:T(8,128)S(1)}, f32[4,1,8,256]{3,2,1,0:T(8,128)S(1)}, u32[]{:S(2)}, u32[]{:S(2)}) collective-permute-start(f32[4,1,8,256]{3,2,1,0:T(8,128)S(1)} %get-tuple-element.205), channel_id=1, source_target_pairs={{0,64},{64,128},{128,192},{192,256},{256,320},{320,384},{384,448},... | collective-permute-start | bytes 98312 | tf_op jit(solution)/shard_map/ppermute | solution.py:35
  51.1 12.5 %collective-permute-start.1 = (f32[4,1,8,256]{3,2,1,0:T(8,128)S(1)}, f32[4,1,8,256]{3,2,1,0:T(8,128)S(1)}, u32[]{:S(2)}, u32[]{:S(2)}) collective-permute-start(f32[4,1,8,256]{3,2,1,0:T(8,128)S(1)} %get-tuple-element.204), channel_id=1, source_target_pairs={{64,0},{128,64},{192,128},{256,192},{320,256},{384,320},{448,384},... | collective-permute-start | bytes 98312 | tf_op jit(solution)/shard_map/ppermute | solution.py:36
  53.2 61.2 %collective-permute-start.2 = (f32[4,16,1,256]{3,2,1,0:T(1,128)}, f32[4,16,1,256]{3,2,1,0:T(1,128)}, u32[]{:S(2)}, u32[]{:S(2)}) collective-permute-start(f32[4,16,1,256]{3,2,1,0:T(1,128)} %get-tuple-element.202), channel_id=1, source_target_pairs={{0,1},{1,2},{2,3},{3,4},{4,5},{5,6},{6,7},{7,8},{8,9},{9,10},{10,1... | collective-permute-start | bytes 196616 | tf_op jit(solution)/shard_map/ppermute | solution.py:35
  57.8 56.6 %collective-permute-start.3 = (f32[4,16,1,256]{3,2,1,0:T(1,128)}, f32[4,16,1,256]{3,2,1,0:T(1,128)}, u32[]{:S(2)}, u32[]{:S(2)}) collective-permute-start(f32[4,16,1,256]{3,2,1,0:T(1,128)} %get-tuple-element.203), channel_id=1, source_target_pairs={{1,0},{2,1},{3,2},{4,3},{5,4},{6,5},{7,6},{8,7},{9,8},{10,9},{11,1... | collective-permute-start | bytes 196616 | tf_op jit(solution)/shard_map/ppermute | solution.py:36
  59.9 5.5 %copy-start.12 = (pred[8]{0:T(512)(128)(4,1)}, pred[8]{0:T(512)(128)(4,1)S(1)}, u32[]{:S(2)}) copy-start(pred[8]{0:T(512)(128)(4,1)S(1)} %get-tuple-element.218) | copy-start | bytes 28
  59.9 5.5 %copy-start.13 = (pred[8]{0:T(512)(128)(4,1)}, pred[8]{0:T(512)(128)(4,1)S(1)}, u32[]{:S(2)}) copy-start(pred[8]{0:T(512)(128)(4,1)S(1)} %get-tuple-element.219) | copy-start | bytes 28
  66.7 3.4 %copy-start.7 = (s32[4096]{0:T(1024)S(1)}, s32[4096]{0:T(1024)}, u32[]{:S(2)}) copy-start(s32[4096]{0:T(1024)} %copy-done.6) | copy-start | bytes 49156
  66.7 3.4 %copy-start.9 = (s32[4096]{0:T(1024)S(1)}, s32[4096]{0:T(1024)}, u32[]{:S(2)}) copy-start(s32[4096]{0:T(1024)} %copy-done.8) | copy-start | bytes 49156
  66.7 3.4 %copy-start.19 = (s32[16]{0:T(128)S(1)}, s32[16]{0:T(128)}, u32[]{:S(2)}) copy-start(s32[16]{0:T(128)} %copy-done.18) | copy-start | bytes 196
  68.1 1.9 %copy-start.11 = (f32[16,4096]{1,0:T(8,128)S(1)}, f32[16,4096]{1,0:T(8,128)}, u32[]{:S(2)}) copy-start(f32[16,4096]{1,0:T(8,128)} %copy-done.10) | copy-start | bytes 786436
  72.3 42.0 %copy-start.1 = (f32[4,16,8,255]{3,2,1,0:T(8,128)S(1)}, f32[4,16,8,255]{3,2,1,0:T(8,128)}, u32[]{:S(2)}) copy-start(f32[4,16,8,255]{3,2,1,0:T(8,128)} %get-tuple-element.192) | copy-start | bytes 1566724
  72.4 42.0 %copy-start.2 = (f32[4,16,8,255]{3,2,1,0:T(8,128)S(1)}, f32[4,16,8,255]{3,2,1,0:T(8,128)}, u32[]{:S(2)}) copy-start(f32[4,16,8,255]{3,2,1,0:T(8,128)} %get-tuple-element.193) | copy-start | bytes 1566724
  72.4 42.0 %copy-start.14 = (pred[16]{0:T(512)(128)(4,1)S(1)}, pred[16]{0:T(512)(128)(4,1)}, u32[]{:S(2)}) copy-start(pred[16]{0:T(512)(128)(4,1)} %get-tuple-element.220) | copy-start | bytes 52
  72.4 42.0 %copy-start.15 = (pred[16]{0:T(512)(128)(4,1)S(1)}, pred[16]{0:T(512)(128)(4,1)}, u32[]{:S(2)}) copy-start(pred[16]{0:T(512)(128)(4,1)} %get-tuple-element.221) | copy-start | bytes 52
  72.4 42.0 %copy-start.16 = (pred[8]{0:T(512)(128)(4,1)S(1)}, pred[8]{0:T(512)(128)(4,1)}, u32[]{:S(2)}) copy-start(pred[8]{0:T(512)(128)(4,1)} %get-tuple-element.216) | copy-start | bytes 28
  72.4 42.0 %copy-start.17 = (pred[8]{0:T(512)(128)(4,1)S(1)}, pred[8]{0:T(512)(128)(4,1)}, u32[]{:S(2)}) copy-start(pred[8]{0:T(512)(128)(4,1)} %get-tuple-element.217) | copy-start | bytes 28
where the time goes:
time: 171 us; the launch traced here: 170 us
  matrix products  55.7 us (33%)
  blocking collectives  50.3 us (29%)
  other arithmetic  27.5 us (16%)
  starting transfers between devices  22.2 us (13%)
  local copies, waits for them, and re-layouts  11.6 us (7%)
  between operations  2.08 us (1%)
    dot_general x8, matrix products, pick_block(): jnp.dot(flat, selector, precision=lax.Precision.HIGHEST, preferred_elemen...  54.2 us
    psum x4, blocking collectives, one_axis_at_a_time(): return functools.reduce(lax.psum, axes, array)  50.3 us
    dynamic_update_slice x4, other arithmetic, march_slab(): picked = lax.map(pick_block, pixel_blocks)  17.8 us
    all_to_all x1, starting transfers between devices, copy_for_each(): lax.all_to_all(jnp.broadcast_to(array[None], (length, *array.shape)), axi...  10.9 us
    ppermute x2, starting transfers between devices, with_halo(): lax.ppermute(last, axis, up)  7.95 us
    unnamed x45, local copies, waits for them, and re-layouts  3.58 us
  transfers between devices with their start and end apart: 5, of which 1 were waited for; matrix products, arithmetic and copies ran while one was open for 32% of the time, Pallas kernels for 0%

commit v1 on v0

v1 whole, which is shorter than its diff:
```python
import functools
import math

import jax
import jax.numpy as jnp
from jax import lax
from jax.experimental import pallas as pl
from jax.experimental.pallas import tpu as pltpu
from jax.sharding import Mesh
from jax.sharding import PartitionSpec as P

STEP = 20
AXES = ("slab", "tile_0", "tile_1", "tile_2")
TILE = AXES[1:]

RENDER_WEIGHT = 1000.0
TV_WEIGHT = 0.05
BACKGROUND = 1.0
STEP_SPAN = 4.0
CLIP_RMS = 0.25
LEARN_RATE = 0.02
BETA_ONE = 0.9
BETA_TWO = 0.99
EPSILON = 1e-08

MESH_ID = pl.DeviceIdType.MESH
F32 = jnp.float32
BF16 = jnp.bfloat16
DEPTH = 16
ROWS = 8
WIDE = 256
KEYS = DEPTH * ROWS
CELLS = 4 * KEYS


def split_bf16(value):
    high = value.astype(BF16)
    return high, (value - high.astype(F32)).astype(BF16)


def sigmoid(value):
    return 1.0 / (1.0 + jnp.exp(-value))


def gradient_kernel(
    sizes,
    step_width,
    grid_hbm,
    pixel_hbm,
    start_hbm,
    count_hbm,
    target_hbm,
    grad_hbm,
    total_ref,
    grid,
    pixel,
    start,
    count,
    target,
    table,
    shade,
    clear,
    share,
    smooth,
    spread,
    grad,
    edge_low,
    edge_high,
    z_low,
    z_high,
    x_low,
    x_high,
    out_part,
    in_part,
    out_cot,
    in_cot,
    mine_a,
    sums_a,
    mine_b,
    sums_b,
    load_sem,
    store_sem,
    halo_send,
    halo_recv,
    part_send,
    part_recv,
    cot_send,
    cot_recv,
    a_send,
    a_recv,
    b_send,
    b_recv,
    ready,
):
    slabs, size_x, size_y, cores = sizes
    group = pixel.shape[1] // slabs
    slab = lax.axis_index("slab")
    at_x = lax.axis_index("tile_0")
    at_y = lax.axis_index("tile_1")
    core = lax.axis_index("tile_2")
    tiles = size_x * size_y * cores
    tile = (at_x * size_y + at_y) * cores + core

    def tile_device(index):
        return (slab, index // (size_y * cores), (index // cores) % size_y, index % cores)

    loads = [
        pltpu.make_async_copy(source, into, load_sem.at[k])
        for k, (source, into) in enumerate(
            (
                (grid_hbm, grid),
                (pixel_hbm, pixel),
                (start_hbm, start),
                (count_hbm, count),
                (target_hbm, target),
            )
        )
    ]
    for load in loads:
        load.start()

    barrier = pltpu.get_barrier_semaphore()
    greeted = 0
    for off in range(1, slabs):
        pl.semaphore_signal(
            barrier,
            inc=1,
            device_id=((slab + off) % slabs, at_x, at_y, core),
            device_id_type=MESH_ID,
        )
        greeted += 1
    for off in range(1, size_x):
        pl.semaphore_signal(
            barrier,
            inc=1,
            device_id=(slab, (at_x + off) % size_x, at_y, core),
            device_id_type=MESH_ID,
        )
        greeted += 1
    for off in range(1, size_y):
        pl.semaphore_signal(
            barrier,
            inc=1,
            device_id=(slab, at_x, (at_y + off) % size_y, core),
            device_id_type=MESH_ID,
        )
        greeted += 1
    for off in (1, tiles - 1):
        pl.semaphore_signal(
            barrier,
            inc=1,
            device_id=tile_device((tile + off) % tiles),
            device_id_type=MESH_ID,
        )
        greeted += 1

    loads[0].wait()
    light = jnp.ones((ROWS, WIDE), F32)
    color = [jnp.zeros((ROWS, WIDE), F32) for _ in range(3)]
    pairs = []
    for z in range(DEPTH):
        raw = grid[pl.ds(z * ROWS, ROWS), :]
        soft = jnp.maximum(raw, 0.0) + jnp.log(1.0 + jnp.exp(-jnp.abs(raw)))
        stay = jnp.exp(-(soft * step_width))
        weight = light * (1.0 - stay)
        light = light * stay
        share[pl.ds(z * ROWS, ROWS), :] = weight
        clear[pl.ds(z * ROWS, ROWS), :] = light
        for c in range(3):
            tone = sigmoid(grid[pl.ds((c + 1) * KEYS + z * ROWS, ROWS), :])
            shade[pl.ds(c * KEYS + z * ROWS, ROWS), :] = tone
            color[c] = color[c] + weight * tone
        pairs.append((*color, 1.0 - light))
        if z % 2:
            for c in range(4):
                high, low = split_bf16(jnp.concatenate([pairs[-2][c], pairs[-1][c]], axis=0))
                rows = pl.ds(c * KEYS + (z - 1) * ROWS, 2 * ROWS)
                table[rows, pl.ds(0, WIDE)] = high
                table[rows, pl.ds(WIDE, WIDE)] = low
    for load in loads[1:]:
        load.wait()

    def partner(place):
        half = (place + 1) // 2
        return (slab + half * (2 * (place % 2) - 1) + slabs) % slabs

    def rays_of(other):
        lanes = pl.ds(pl.multiple_of(other * group, group), group)
        cell = pixel[:, lanes]
        begin = start[:, lanes]
        taken = begin * DEPTH + count[:, lanes] - slab * DEPTH
        taken = jnp.where(begin <= slab, jnp.clip(taken, 0, DEPTH), 0)
        key = (taken - 1) * ROWS + cell // WIDE
        across = lax.broadcasted_iota(jnp.int32, (WIDE, group), 0)
        column = jnp.where(across == cell % WIDE, 1.0, 0.0).astype(BF16)
        return key, column

    def part_copy(other):
        return pltpu.make_async_remote_copy(
            src_ref=out_part.at[other],
            dst_ref=in_part.at[slab],
            send_sem=part_send.at[other],
            recv_sem=part_recv.at[slab],
            device_id=(other, at_x, at_y, core),
            device_id_type=MESH_ID,
        )

    def part_arrival(other):
        return pltpu.make_async_remote_copy(
            src_ref=out_part.at[other],
            dst_ref=in_part.at[other],
            send_sem=part_send.at[other],
            recv_sem=part_recv.at[other],
            device_id=(other, at_x, at_y, core),
            device_id_type=MESH_ID,
        )

    def look_up(other):
        key, column = rays_of(other)
        found = jnp.dot(
            table[...],
            jnp.concatenate([column, column], axis=0),
            preferred_element_type=F32,
        )
        chosen = lax.broadcasted_iota(jnp.int32, (KEYS, group), 0) == key
        values = [
            jnp.sum(
                jnp.where(chosen, found[c * KEYS : (c + 1) * KEYS], 0.0),
                axis=0,
                keepdims=True,
            )
            for c in range(4)
        ]
        values[3] = 1.0 - values[3]
        return jnp.concatenate(values, axis=0)

    def look_up_and_send(order, carry):
        other = partner(slabs - 1 - order)
        out_part[other] = look_up(other)

        @pl.when(order == 0)
        def _():
            pl.semaphore_wait(barrier, greeted)

        part_copy(other).start()
        return carry

    lax.fori_loop(0, slabs - 1, look_up_and_send, 0)
    in_part[slab] = look_up(slab)

    for off in range(1, size_y):
        pl.semaphore_signal(
            ready,
            inc=1,
            device_id=(slab, at_x, (at_y + off) % size_y, core),
            device_id_type=MESH_ID,
        )
    for k in range(CELLS // ROWS):
        edge_low[pl.ds(k, 1), :] = grid[pl.ds(k * ROWS, 1), :]
        edge_high[pl.ds(k, 1), :] = grid[pl.ds(k * ROWS + ROWS - 1, 1), :]
    next_slab = ((slab + 1) % slabs, at_x, at_y, core)
    prev_slab = ((slab + slabs - 1) % slabs, at_x, at_y, core)
    next_tile = tile_device((tile + 1) % tiles)
    prev_tile = tile_device((tile + tiles - 1) % tiles)
    halos = []
    for c in range(4):
        last = grid.at[pl.ds(c * KEYS + (DEPTH - 1) * ROWS, ROWS)]
        first = grid.at[pl.ds(c * KEYS, ROWS)]
        halos.append((last, z_low.at[c], next_slab))
        halos.append((first, z_high.at[c], prev_slab))
    halos.append((edge_high, x_low, next_tile))
    halos.append((edge_low, x_high, prev_tile))
    halos = [
        pltpu.make_async_remote_copy(
            src_ref=source,
            dst_ref=into,
            send_sem=halo_send.at[k],
            recv_sem=halo_recv.at[k],
            device_id=device,
            device_id_type=MESH_ID,
        )
        for k, (source, into, device) in enumerate(halos)
    ]
    for halo in halos:
        halo.start()
    for halo in halos:
        halo.wait()

    row_at = lax.broadcasted_iota(jnp.int32, (ROWS, WIDE), 0)
    lane_at = lax.broadcasted_iota(jnp.int32, (ROWS, WIDE), 1)

    def smooth_channel(c, carry):
        base = c * KEYS
        for z in range(DEPTH):
            here = pl.ds(pl.multiple_of(base + z * ROWS, ROWS), ROWS)
            value = grid[here, :]
            if z > 0:
                total = value - grid[pl.ds(pl.multiple_of(base + (z - 1) * ROWS, ROWS), ROWS), :]
            else:
                total = jnp.where(slab > 0, value - z_low[c], 0.0)
            if z < DEPTH - 1:
                total += value - grid[pl.ds(pl.multiple_of(base + (z + 1) * ROWS, ROWS), ROWS), :]
            else:
                total += jnp.where(slab < slabs - 1, value - z_high[c], 0.0)
            below = jnp.where(
                row_at == 0, x_low[pl.ds(c * DEPTH + z, 1), :], pltpu.roll(value, 1, 0)
            )
            above = jnp.where(
                row_at == ROWS - 1,
                x_high[pl.ds(c * DEPTH + z, 1), :],
                pltpu.roll(value, ROWS - 1, 0),
            )
            total += jnp.where((row_at > 0) | (tile > 0), value - below, 0.0)
            total += jnp.where((row_at < ROWS - 1) | (tile < tiles - 1), value - above, 0.0)
            total += jnp.where(lane_at > 0, value - pltpu.roll(value, 1, 1), 0.0)
            total += jnp.where(lane_at < WIDE - 1, value - pltpu.roll(value, WIDE - 1, 1), 0.0)
            smooth[here, :] = (2.0 * TV_WEIGHT) * total
        return carry

    lax.fori_loop(0, 4, smooth_channel, 0)

    def await_part(order, carry):
        part_arrival(partner(order)).wait_recv()
        return carry

    lax.fori_loop(1, slabs, await_part, 0)
    goal = target[:, pl.ds(pl.multiple_of(slab * group, group), group)]
    ahead = jnp.ones((1, group), F32)
    rendered = jnp.zeros((3, group), F32)
    reach = []
    for s in range(slabs):
        reach.append(ahead)
        part = in_part[s]
        rendered = rendered + ahead * part[:3]
        ahead = ahead * part[3:]
    residual = RENDER_WEIGHT * (rendered + ahead * BACKGROUND - goal)
    beyond = jnp.full((3, group), BACKGROUND, F32)
    for s in range(slabs - 1, -1, -1):
        product = residual * beyond
        dark = product[0:1] + product[1:2] + product[2:3]
        out_cot[s] = reach[s] * jnp.concatenate([residual, dark], axis=0)
        part = in_part[s]
        beyond = part[:3] + part[3:] * beyond

    def cot_copy(other):
        return pltpu.make_async_remote_copy(
            src_ref=out_cot.at[other],
            dst_ref=in_cot.at[slab],
            send_sem=cot_send.at[other],
            recv_sem=cot_recv.at[slab],
            device_id=(other, at_x, at_y, core),
            device_id_type=MESH_ID,
        )

    def cot_arrival(other):
        return pltpu.make_async_remote_copy(
            src_ref=out_cot.at[other],
            dst_ref=in_cot.at[other],
            send_sem=cot_send.at[other],
            recv_sem=cot_recv.at[other],
            device_id=(other, at_x, at_y, core),
            device_id_type=MESH_ID,
        )

    def send_cot(order, carry):
        cot_copy(partner(slabs - 1 - order)).start()
        return carry

    lax.fori_loop(0, slabs - 1, send_cot, 0)
    in_cot[slab] = out_cot[slab]
    spread[...] = jnp.zeros_like(spread)

    def scatter(order, carry):
        other = partner(order)

        @pl.when(order > 0)
        def _():
            cot_arrival(other).wait_recv()

        key, column = rays_of(other)
        chosen = jnp.where(
            lax.broadcasted_iota(jnp.int32, (KEYS, group), 0) == key, 1.0, 0.0
        ).astype(BF16)
        cot = in_cot[other]
        high, low = split_bf16(cot)
        left = jnp.concatenate(
            [
                jnp.concatenate([chosen * high[c : c + 1], chosen * low[c : c + 1]], axis=1)
                for c in range(4)
            ],
            axis=0,
        )
        spread[...] += lax.dot_general(
            left,
            jnp.concatenate([column, column], axis=1),
            (((1,), (1,)), ((), ())),
            preferred_element_type=F32,
        )
        return carry

    lax.fori_loop(0, slabs, scatter, 0)

    later = [jnp.zeros((ROWS, WIDE), F32) for _ in range(3)]
    tail = jnp.zeros((ROWS, WIDE), F32)
    squares = jnp.zeros((ROWS, WIDE), F32)
    for z in range(DEPTH - 1, -1, -1):
        here = pl.ds(z * ROWS, ROWS)
        weight = share[here, :]
        light = clear[here, :]
        pull = jnp.zeros((ROWS, WIDE), F32)
        for c in range(3):
            rows = pl.ds(c * KEYS + z * ROWS, ROWS)
            tone = shade[rows, :]
            later[c] = later[c] + spread[rows, :]
            pull = pull + tone * later[c]
            rows = pl.ds((c + 1) * KEYS + z * ROWS, ROWS)
            value = weight * later[c] * (tone * (1.0 - tone)) + smooth[rows, :]
            grad[rows, :] = value
            squares = squares + value * value
        tail = tail + spread[pl.ds(3 * KEYS + z * ROWS, ROWS), :] * light
        thick = pull * light - tail
        tail = tail + pull * weight
        value = thick * (step_width * sigmoid(grid[here, :])) + smooth[here, :]
        grad[here, :] = value
        squares = squares + value * value
    out_copy = pltpu.make_async_copy(grad, grad_hbm, store_sem)
    out_copy.start()

    squares = squares[:, :128] + squares[:, 128:]
    own = jnp.sum(squares, axis=0, keepdims=True)
    mine_a[...] = own
    n_a = slabs * cores
    me_a = slab * cores + core

    def a_copy(off, slot):
        to = (me_a + off) % n_a
        return pltpu.make_async_remote_copy(
            src_ref=mine_a,
            dst_ref=sums_a.at[slot],
            send_sem=a_send.at[off],
            recv_sem=a_recv.at[slot],
            device_id=(to // cores, at_x, at_y, to % cores),
            device_id_type=MESH_ID,
        )

    def each(first, last, do):
        def body(k, carry):
            do(k)
            return carry

        lax.fori_loop(first, last, body, 0)

    each(1, n_a, lambda off: a_copy(off, me_a).start())
    sums_a[me_a] = own
    each(1, n_a, lambda off: a_copy(off, (me_a + off) % n_a).wait_recv())
    own = jnp.sum(sums_a[...], axis=0)
    mine_b[...] = own
    n_b = size_x * size_y
    me_b = at_x * size_y + at_y

    def b_copy(off, slot):
        to = (me_b + off) % n_b
        return pltpu.make_async_remote_copy(
            src_ref=mine_b,
            dst_ref=sums_b.at[slot],
            send_sem=b_send.at[off],
            recv_sem=b_recv.at[slot],
            device_id=(slab, to // size_y, to % size_y, core),
            device_id_type=MESH_ID,
        )

    if size_y > 1:
        pl.semaphore_wait(ready, size_y - 1)
    each(1, n_b, lambda off: b_copy(off, me_b).start())
    sums_b[me_b] = own
    each(1, n_b, lambda off: b_copy(off, (me_b + off) % n_b).wait_recv())
    total_ref[...] = jnp.sum(sums_b[...], axis=0)

    each(1, slabs, lambda k: part_copy(partner(k)).wait_send())
    each(1, slabs, lambda k: cot_copy(partner(k)).wait_send())
    each(1, n_a, lambda off: a_copy(off, me_a).wait_send())
    each(1, n_b, lambda off: b_copy(off, me_b).wait_send())
    out_copy.wait()


def update_kernel(limit, grid_ref, first_ref, second_ref, grad_ref, total_ref, *outs):
    new_grid, new_first, new_second = outs
    norm = jnp.sqrt(jnp.sum(total_ref[...], axis=1, keepdims=True))
    scale = limit / jnp.maximum(norm, limit)
    clipped = grad_ref[...] * scale
    first = BETA_ONE * first_ref[...] + (1.0 - BETA_ONE) * clipped
    second = BETA_TWO * second_ref[...] + (1.0 - BETA_TWO) * clipped * clipped
    new_first[...] = first
    new_second[...] = second
    first_hat = first * (1.0 / (1.0 - BETA_ONE**STEP))
    second_hat = second * (1.0 / (1.0 - BETA_TWO**STEP))
    new_grid[...] = grid_ref[...] - LEARN_RATE * first_hat / (jnp.sqrt(second_hat) + EPSILON)


def per_device(voxel_grid, first_moment, second_moment, pixel_index, start_slab, ray_count, target):
    sizes = tuple(lax.axis_size(axis) for axis in AXES)
    slabs = sizes[0]
    rays = pixel_index.shape[0]
    group = rays // slabs
    total_depth = DEPTH * slabs
    total_x = ROWS * math.prod(sizes[1:])
    n_a = slabs * sizes[3]
    n_b = sizes[1] * sizes[2]
    flat = (CELLS, WIDE)
    dma = pltpu.SemaphoreType.DMA
    anywhere = pl.BlockSpec(memory_space=pl.ANY)
    grad, total = pl.pallas_call(
        functools.partial(gradient_kernel, sizes, STEP_SPAN / total_depth),
        out_shape=(
            jax.ShapeDtypeStruct(flat, F32),
            jax.ShapeDtypeStruct((1, 128), F32),
        ),
        in_specs=[anywhere] * 5,
        out_specs=(anywhere, pl.BlockSpec(memory_space=pltpu.VMEM)),
        scratch_shapes=[
            pltpu.VMEM(flat, F32),
            pltpu.VMEM((1, rays), jnp.int32),
            pltpu.VMEM((1, rays), jnp.int32),
            pltpu.VMEM((1, rays), jnp.int32),
            pltpu.VMEM((3, rays), F32),
            pltpu.VMEM((CELLS, 2 * WIDE), BF16),
            pltpu.VMEM((3 * KEYS, WIDE), F32),
            pltpu.VMEM((KEYS, WIDE), F32),
            pltpu.VMEM((KEYS, WIDE), F32),
            pltpu.VMEM(flat, F32),
            pltpu.VMEM(flat, F32),
            pltpu.VMEM(flat, F32),
            pltpu.VMEM((CELLS // ROWS, WIDE), F32),
            pltpu.VMEM((CELLS // ROWS, WIDE), F32),
            pltpu.VMEM((4, ROWS, WIDE), F32),
            pltpu.VMEM((4, ROWS, WIDE), F32),
            pltpu.VMEM((CELLS // ROWS, WIDE), F32),
            pltpu.VMEM((CELLS // ROWS, WIDE), F32),
            pltpu.VMEM((slabs, 4, group), F32),
            pltpu.VMEM((slabs, 4, group), F32),
            pltpu.VMEM((slabs, 4, group), F32),
            pltpu.VMEM((slabs, 4, group), F32),
            pltpu.VMEM((1, 128), F32),
            pltpu.VMEM((n_a, 1, 128), F32),
            pltpu.VMEM((1, 128), F32),
            pltpu.VMEM((n_b, 1, 128), F32),
            dma((5,)),
            dma,
            dma((10,)),
            dma((10,)),
            dma((slabs,)),
            dma((slabs,)),
            dma((slabs,)),
            dma((slabs,)),
            dma((n_a,)),
            dma((n_a,)),
            dma((n_b,)),
            dma((n_b,)),
            pltpu.SemaphoreType.REGULAR,
        ],
        compiler_params=pltpu.CompilerParams(collective_id=0, has_side_effects=True),
        name="render_gradient",
    )(
        voxel_grid.reshape(flat),
        pixel_index.reshape(1, rays),
        start_slab.reshape(1, rays),
        ray_count.reshape(1, rays),
        target,
    )
    limit = CLIP_RMS * math.sqrt(4.0 * total_depth * total_x * WIDE)
    block = pl.BlockSpec((KEYS, WIDE), lambda i: (i, 0))
    outs = pl.pallas_call(
        functools.partial(update_kernel, limit),
        grid=(4,),
        out_shape=[jax.ShapeDtypeStruct(flat, F32)] * 3,
        in_specs=[block] * 4 + [pl.BlockSpec((1, 128), lambda i: (0, 0))],
        out_specs=[block] * 3,
        name="clipped_adam",
    )(
        voxel_grid.reshape(flat),
        first_moment.reshape(flat),
        second_moment.reshape(flat),
        grad,
        total,
    )
    return tuple(out.reshape(voxel_grid.shape) for out in outs)


def solution(mesh):
    torus = Mesh(mesh.devices.reshape(mesh.shape["slab"], 4, 8, 2), AXES)
    cells = P(None, "slab", TILE, None)
    rays = P(TILE)
    return jax.shard_map(
        per_device,
        mesh=torus,
        in_specs=(cells, cells, cells, rays, rays, rays, P(None, TILE)),
        out_specs=(cells, cells, cells),
        check_vma=False,
    )
```

time: 171 us -> 47.5 us (0.28)
  matrix products: 55.7 us -> 0 us
  blocking collectives: 50.3 us -> 0 us
  Pallas kernels: 0 us -> 46.6 us
  other arithmetic: 27.5 us -> 0 us
  starting transfers between devices: 22.2 us -> 0 us
  local copies, waits for them, and re-layouts: 11.6 us -> 0 us
    dot_general x10 -> x0, matrix products: 55.7 us -> none  [the longest x8 54.2 us: pick_block(): jnp.dot(flat, selector, precision=lax.Precision.HIGHEST, preferred_elemen...]
    psum x4 -> x0, blocking collectives: 50.3 us -> none  [one_axis_at_a_time(): return functools.reduce(lax.psum, axes, array)]
    pallas_call x0 -> x2, Pallas kernels: none -> 46.6 us  [the longest x1 42.6 us: per_device(): pl.pallas_call(functools.partial(gradient_kernel, sizes, STEP_SPAN / tota...]
    dynamic_update_slice x4 -> x0, other arithmetic: 17.8 us -> none  [march_slab(): picked = lax.map(pick_block, pixel_blocks)]
    ppermute x4 -> x0, starting transfers between devices: 11.3 us -> none  [the longest x2 7.95 us: with_halo(): lax.ppermute(last, axis, up)]
    all_to_all x1 -> x0, starting transfers between devices: 10.9 us -> none  [copy_for_each(): lax.all_to_all(jnp.broadcast_to(array[None], (length, *array.shape)), axi...]
    unnamed x45 -> x0, local copies, waits for them, and re-layouts: 3.58 us -> none
    slice x14 -> x0, local copies, waits for them, and re-layouts: 3.42 us -> none  [the longest x11 2.54 us: combined_pairwise(): part[side::2]]
  transfers between devices with their start and end apart: 5 -> 0, of which waited for: 1 -> 0; matrix products, arithmetic and copies ran while one was open for 32% -> 0% of each run, Pallas kernels for 0% -> 0%
where the time goes in v1:
time: 47.5 us; the launch traced here: 47.3 us
  Pallas kernels  46.6 us (98%)
  between operations  0.64 us (1%)
    pallas_call x1, Pallas kernels, per_device(): pl.pallas_call(functools.partial(gradient_kernel, sizes, STEP_SPAN / tota...  42.6 us
    pallas_call x1, Pallas kernels, per_device(): pl.pallas_call(functools.partial(update_kernel, limit), grid=(4,), out_sh...  3.98 us

profile of v1, /device:TPU:1, one launch (start us, length us, event | category | flops | bytes accessed | tf_op | source)
XLA Modules:
  0.0 47.3 jit_solution(1085025295039467360)
XLA Ops:
  0.6 42.6 %render_gradient.1 = (f32[512,256]{1,0:T(8,128)}, f32[1,128]{1,0:T(1,128)}) custom-call(f32[512,256]{1,0:T(8,128)} %bitcast.9, s32[1,4096]{1,0:T(1,128)} %bitcast.13, s32[1,4096]{1,0:T(1,128)} %bitcast.14, s32[1,4096]{1,0:T(1,128)} %bitcast.15, f32[3,4096]{1,0:T(4,128)} %target_hbm.1), custom_call_target="tpu_custom_call" | custom-call | tf_op jit(solution)/shard_map/render_gradient/pallas_call | solution.py:512
  43.3 4.0 %clipped_adam.1 = (f32[512,256]{1,0:T(8,128)}, f32[512,256]{1,0:T(8,128)}, f32[512,256]{1,0:T(8,128)}) custom-call(f32[512,256]{1,0:T(8,128)} %bitcast.10, f32[512,256]{1,0:T(8,128)} %bitcast.11, f32[512,256]{1,0:T(8,128)} %bitcast.12, f32[512,256]{1,0:T(8,128)} %get-tuple-element.8.grad_ref, f32[1,128]{1,0:T(1,128)} %get-tuple-element.9.total_ref), custom_call_target="tpu_custom_call" | custom-call | tf_op jit(solution)/shard_map/clipped_adam/pallas_call | solution.py:572

commit v2 on v1

v2 whole, which is shorter than its diff:
```python
import functools
import math

import jax
import jax.numpy as jnp
from jax import lax
from jax.experimental import pallas as pl
from jax.experimental.pallas import tpu as pltpu
from jax.sharding import Mesh
from jax.sharding import PartitionSpec as P

STEP = 20
AXES = ("slab", "tile_0", "tile_1", "tile_2")
TILE = AXES[1:]

RENDER_WEIGHT = 1000.0
TV_WEIGHT = 0.05
BACKGROUND = 1.0
STEP_SPAN = 4.0
CLIP_RMS = 0.25
LEARN_RATE = 0.02
BETA_ONE = 0.9
BETA_TWO = 0.99
EPSILON = 1e-08

MESH_ID = pl.DeviceIdType.MESH
F32 = jnp.float32
BF16 = jnp.bfloat16
DEPTH = 16
ROWS = 8
WIDE = 256
KEYS = DEPTH * ROWS
CELLS = 4 * KEYS


def split_bf16(value):
    high = value.astype(BF16)
    return high, (value - high.astype(F32)).astype(BF16)


def sigmoid(value):
    return 1.0 / (1.0 + jnp.exp(-value))


def gradient_kernel(
    sizes,
    step_width,
    grid_hbm,
    first_hbm,
    second_hbm,
    pixel_hbm,
    start_hbm,
    count_hbm,
    target_hbm,
    grid,
    first,
    second,
    grad,
    total_ref,
    pixel,
    start,
    count,
    target,
    table,
    shade,
    clear,
    share,
    smooth,
    spread,
    columns,
    chosens,
    edges,
    halo,
    out_part,
    in_part,
    out_cot,
    in_cot,
    mine,
    sums_a,
    sums_b,
    grid_sem,
    rays_sem,
    moment_sem,
    halo_sem,
    part_sem,
    cot_send,
    cot_recv,
    a_sem,
    b_sem,
    ready,
):
    slabs, size_x, size_y, cores = sizes
    group = pixel.shape[1] // slabs
    slab = lax.axis_index("slab")
    at_x = lax.axis_index("tile_0")
    at_y = lax.axis_index("tile_1")
    core = lax.axis_index("tile_2")
    tiles = size_x * size_y * cores
    tile = (at_x * size_y + at_y) * cores + core
    n_a = slabs * cores
    n_b = size_x * size_y

    def remote(source, into, send, recv, device):
        return pltpu.make_async_remote_copy(
            src_ref=source,
            dst_ref=into,
            send_sem=send,
            recv_sem=recv,
            device_id=device,
            device_id_type=MESH_ID,
        )

    def signal(semaphore, device):
        pl.semaphore_signal(semaphore, inc=1, device_id=device, device_id_type=MESH_ID)

    def tile_device(index):
        return (slab, index // (size_y * cores), (index // cores) % size_y, index % cores)

    def far_first(size):
        return sorted(range(1, size), key=lambda off: -min(off, size - off))

    over_a = [(z, c) for z in far_first(slabs) + [0] for c in range(cores) if z or c]
    over_b = sorted(
        ((x, y) for x in range(size_x) for y in range(size_y) if x or y),
        key=lambda off: -min(off[0], size_x - off[0]) - min(off[1], size_y - off[1]),
    )

    def device_a(off):
        return ((slab + off[0]) % slabs, at_x, at_y, (core + off[1]) % cores)

    def device_b(off):
        return (slab, (at_x + off[0]) % size_x, (at_y + off[1]) % size_y, core)

    barrier = pltpu.get_barrier_semaphore()
    greet = [device_a(off) for off in over_a]
    greet += [device_b((0, y)) for y in far_first(size_y)]
    greet += [device_b((x, 0)) for x in far_first(size_x)]
    next_tile = tile_device((tile + 1) % tiles)
    prev_tile = tile_device((tile + tiles - 1) % tiles)
    greet += [next_tile, prev_tile]

    load_grid = pltpu.make_async_copy(grid_hbm, grid, grid_sem)
    load_grid.start()
    for device in greet:
        signal(barrier, device)
    ray_loads = [
        pltpu.make_async_copy(source, into, rays_sem.at[k])
        for k, (source, into) in enumerate(
            ((pixel_hbm, pixel), (start_hbm, start), (count_hbm, count), (target_hbm, target))
        )
    ]
    for load in ray_loads:
        load.start()
    moment_loads = [
        pltpu.make_async_copy(first_hbm, first, moment_sem.at[0]),
        pltpu.make_async_copy(second_hbm, second, moment_sem.at[1]),
    ]
    for load in moment_loads:
        load.start()

    load_grid.wait()
    light = jnp.ones((ROWS, WIDE), F32)
    color = [jnp.zeros((ROWS, WIDE), F32) for _ in range(3)]
    pairs = []
    for z in range(DEPTH):
        raw = grid[0, z]
        soft = jnp.maximum(raw, 0.0) + jnp.log(1.0 + jnp.exp(-jnp.abs(raw)))
        stay = jnp.exp(-(soft * step_width))
        weight = light * (1.0 - stay)
        light = light * stay
        share[z] = weight
        clear[z] = light
        for c in range(3):
            tone = sigmoid(grid[c + 1, z])
            shade[c, z] = tone
            color[c] = color[c] + weight * tone
        pairs.append((*color, 1.0 - light))
        if z % 2:
            for c in range(4):
                high, low = split_bf16(jnp.concatenate([pairs[-2][c], pairs[-1][c]], axis=0))
                rows = pl.ds(c * KEYS + (z - 1) * ROWS, 2 * ROWS)
                table[rows, pl.ds(0, WIDE)] = high
                table[rows, pl.ds(WIDE, WIDE)] = low
    for load in ray_loads:
        load.wait()

    def partner(place):
        half = (place + 1) // 2
        return (slab + half * (2 * (place % 2) - 1) + slabs) % slabs

    def ring(other):
        return (other, at_x, at_y, core)

    def look_up(other):
        lanes = pl.ds(pl.multiple_of(other * group, group), group)
        cell = pixel[:, lanes]
        begin = start[:, lanes]
        taken = begin * DEPTH + count[:, lanes] - slab * DEPTH
        taken = jnp.where(begin <= slab, jnp.clip(taken, 0, DEPTH), 0)
        key = (taken - 1) * ROWS + cell // WIDE
        across = lax.broadcasted_iota(jnp.int32, (WIDE, group), 0)
        column = jnp.where(across == cell % WIDE, 1.0, 0.0).astype(BF16)
        columns[other] = column
        found = jnp.dot(
            table[...],
            jnp.concatenate([column, column], axis=0),
            preferred_element_type=F32,
        )
        chosen = lax.broadcasted_iota(jnp.int32, (KEYS, group), 0) == key
        chosens[other] = jnp.where(chosen, 1.0, 0.0).astype(BF16)
        values = [
            jnp.sum(
                jnp.where(chosen, found[c * KEYS : (c + 1) * KEYS], 0.0),
                axis=0,
                keepdims=True,
            )
            for c in range(4)
        ]
        values[3] = 1.0 - values[3]
        return jnp.concatenate(values, axis=0)

    def send_part(other):
        remote(
            out_part.at[other], in_part.at[slab], part_sem.at[0], part_sem.at[1], ring(other)
        ).start()

    places = list(range(slabs - 1, 0, -1))
    early = places[: slabs // 2]
    for place in early:
        out_part[partner(place)] = look_up(partner(place))
    pl.semaphore_wait(barrier, len(greet))
    for place in early:
        send_part(partner(place))
    for place in places[slabs // 2 :]:
        out_part[partner(place)] = look_up(partner(place))
        send_part(partner(place))
    in_part[slab] = look_up(slab)

    for off in far_first(size_y):
        signal(ready, device_b((0, off)))
    for c in range(4):
        for z in range(DEPTH):
            k = c * DEPTH + z
            edges[0, k // ROWS, pl.ds(k % ROWS, 1), :] = grid[c, z, pl.ds(ROWS - 1, 1), :]
            edges[1, k // ROWS, pl.ds(k % ROWS, 1), :] = grid[c, z, pl.ds(0, 1), :]
    for source, into, device in (
        (edges.at[0], halo.at[pl.ds(8, 8)], next_tile),
        (edges.at[1], halo.at[pl.ds(16, 8)], prev_tile),
        (grid.at[:, DEPTH - 1], halo.at[pl.ds(0, 4)], device_a((1, 0))),
        (grid.at[:, 0], halo.at[pl.ds(4, 4)], device_a((slabs - 1, 0))),
    ):
        remote(source, into, halo_sem.at[0], halo_sem.at[1], device).start()

    others = pl.ds(0, slabs - 1)
    all_parts = remote(
        out_part.at[others], in_part.at[others], part_sem.at[0], part_sem.at[1], ring(slab)
    )
    goal = target[:, pl.ds(pl.multiple_of(slab * group, group), group)]
    all_parts.wait_recv()
    ahead = jnp.ones((1, group), F32)
    rendered = jnp.zeros((3, group), F32)
    reach = []
    for s in range(slabs):
        reach.append(ahead)
        part = in_part[s]
        rendered = rendered + ahead * part[:3]
        ahead = ahead * part[3:]
    residual = RENDER_WEIGHT * (rendered + ahead * BACKGROUND - goal)
    beyond = jnp.full((3, group), BACKGROUND, F32)
    for s in range(slabs - 1, -1, -1):
        product = residual * beyond
        dark = product[0:1] + product[1:2] + product[2:3]
        out_cot[s] = reach[s] * jnp.concatenate([residual, dark], axis=0)
        part = in_part[s]
        beyond = part[:3] + part[3:] * beyond

    for place in places:
        other = partner(place)
        remote(
            out_cot.at[other], in_cot.at[slab], cot_send, cot_recv.at[slab], ring(other)
        ).start()

    def scatter(other, cot):
        high, low = split_bf16(cot)
        chosen = chosens[other]
        column = columns[other]
        left = jnp.concatenate(
            [
                jnp.concatenate([chosen * high[c : c + 1], chosen * low[c : c + 1]], axis=1)
                for c in range(4)
            ],
            axis=0,
        )
        return lax.dot_general(
            left,
            jnp.concatenate([column, column], axis=1),
            (((1,), (1,)), ((), ())),
            preferred_element_type=F32,
        )

    spread[...] = scatter(slab, out_cot[slab])

    remote(halo, halo, halo_sem.at[0], halo_sem.at[1], next_tile).wait()
    row_at = lax.broadcasted_iota(jnp.int32, (ROWS, WIDE), 0)
    lane_at = lax.broadcasted_iota(jnp.int32, (ROWS, WIDE), 1)

    def smooth_channel(c, carry):
        for z in range(DEPTH):
            value = grid[c, z]
            if z > 0:
                total = value - grid[c, z - 1]
            else:
                total = jnp.where(slab > 0, value - halo[c], 0.0)
            if z < DEPTH - 1:
                total += value - grid[c, z + 1]
            else:
                total += jnp.where(slab < slabs - 1, value - halo[4 + c], 0.0)
            line = (2 * c + z // ROWS, pl.ds(z % ROWS, 1), slice(None))
            below = jnp.where(
                row_at == 0, halo[8 + line[0], line[1], line[2]], pltpu.roll(value, 1, 0)
            )
            above = jnp.where(
                row_at == ROWS - 1,
                halo[16 + line[0], line[1], line[2]],
                pltpu.roll(value, ROWS - 1, 0),
            )
            total += jnp.where((row_at > 0) | (tile > 0), value - below, 0.0)
            total += jnp.where((row_at < ROWS - 1) | (tile < tiles - 1), value - above, 0.0)
            total += jnp.where(lane_at > 0, value - pltpu.roll(value, 1, 1), 0.0)
            total += jnp.where(lane_at < WIDE - 1, value - pltpu.roll(value, WIDE - 1, 1), 0.0)
            smooth[c, z] = (2.0 * TV_WEIGHT) * total
        return carry

    lax.fori_loop(0, 4, smooth_channel, 0)

    def scatter_arrived(place, carry):
        other = partner(place)
        remote(
            out_cot.at[other], in_cot.at[other], cot_send, cot_recv.at[other], ring(other)
        ).wait_recv()
        spread[...] += scatter(other, in_cot[other])
        return carry

    lax.fori_loop(1, slabs, scatter_arrived, 0)

    later = [jnp.zeros((ROWS, WIDE), F32) for _ in range(3)]
    tail = jnp.zeros((ROWS, WIDE), F32)
    squares = jnp.zeros((ROWS, WIDE), F32)
    for z in range(DEPTH - 1, -1, -1):
        weight = share[z]
        light = clear[z]
        pull = jnp.zeros((ROWS, WIDE), F32)
        for c in range(3):
            tone = shade[c, z]
            later[c] = later[c] + spread[pl.ds(c * KEYS + z * ROWS, ROWS), :]
            pull = pull + tone * later[c]
            value = weight * later[c] * (tone * (1.0 - tone)) + smooth[c + 1, z]
            grad[c + 1, z] = value
            squares = squares + value * value
        tail = tail + spread[pl.ds(3 * KEYS + z * ROWS, ROWS), :] * light
        thick = pull * light - tail
        tail = tail + pull * weight
        value = thick * (step_width * sigmoid(grid[0, z])) + smooth[0, z]
        grad[0, z] = value
        squares = squares + value * value

    squares = squares[:, :128] + squares[:, 128:]
    own = jnp.sum(squares, axis=0, keepdims=True)
    mine[0] = own
    me_a = slab * cores + core
    for off in over_a:
        remote(mine.at[0], sums_a.at[me_a], a_sem.at[0], a_sem.at[1], device_a(off)).start()
    sums_a[me_a] = own
    all_parts.wait_send()
    remote(
        out_cot.at[others], in_cot.at[others], cot_send, cot_recv.at[0], ring(slab)
    ).wait_send()
    for load in moment_loads:
        load.wait()
    if size_y > 1:
        pl.semaphore_wait(ready, size_y - 1)
    some = sums_a.at[pl.ds(0, n_a - 1)]
    remote(some, some, a_sem.at[0], a_sem.at[1], next_tile).wait()
    own = jnp.sum(sums_a[...], axis=0)
    mine[1] = own
    me_b = at_x * size_y + at_y
    for off in over_b:
        remote(mine.at[1], sums_b.at[me_b], b_sem.at[0], b_sem.at[1], device_b(off)).start()
    sums_b[me_b] = own
    some = sums_b.at[pl.ds(0, n_b - 1)]
    remote(some, some, b_sem.at[0], b_sem.at[1], next_tile).wait()
    total_ref[...] = jnp.sum(sums_b[...], axis=0)


def update_kernel(limit, grid, first, second, grad, total, *rest):
    outs, held, sem = rest[:3], rest[3:6], rest[6]
    norm = jnp.sqrt(jnp.sum(total[...], axis=1, keepdims=True))
    scale = limit / jnp.maximum(norm, limit)
    for c in range(4):
        clipped = grad[c] * scale
        new_first = BETA_ONE * first[c] + (1.0 - BETA_ONE) * clipped
        new_second = BETA_TWO * second[c] + (1.0 - BETA_TWO) * clipped * clipped
        held[1][c] = new_first
        held[2][c] = new_second
        first_hat = new_first * (1.0 / (1.0 - BETA_ONE**STEP))
        second_hat = new_second * (1.0 / (1.0 - BETA_TWO**STEP))
        held[0][c] = grid[c] - LEARN_RATE * first_hat / (jnp.sqrt(second_hat) + EPSILON)
        for k in range(3):
            pltpu.make_async_copy(held[k].at[c], outs[k].at[c], sem.at[k]).start()
    for k in range(3):
        pltpu.make_async_copy(held[k], outs[k], sem.at[k]).wait()


def per_device(voxel_grid, first_moment, second_moment, pixel_index, start_slab, ray_count, target):
    sizes = tuple(lax.axis_size(axis) for axis in AXES)
    slabs = sizes[0]
    rays = pixel_index.shape[0]
    group = rays // slabs
    total_depth = DEPTH * slabs
    total_x = ROWS * math.prod(sizes[1:])
    n_a = slabs * sizes[3]
    n_b = sizes[1] * sizes[2]
    block = (4, DEPTH, ROWS, WIDE)
    dma = pltpu.SemaphoreType.DMA
    anywhere = pl.BlockSpec(memory_space=pl.ANY)
    inside = pl.BlockSpec(memory_space=pltpu.VMEM)
    held = pltpu.VMEM(block, F32)
    grid, first, second, grad, total = pl.pallas_call(
        functools.partial(gradient_kernel, sizes, STEP_SPAN / total_depth),
        out_shape=(held, held, held, held, pltpu.VMEM((1, 128), F32)),
        in_specs=[anywhere] * 7,
        out_specs=(inside,) * 5,
        scratch_shapes=[
            pltpu.VMEM((1, rays), jnp.int32),
            pltpu.VMEM((1, rays), jnp.int32),
            pltpu.VMEM((1, rays), jnp.int32),
            pltpu.VMEM((3, rays), F32),
            pltpu.VMEM((CELLS, 2 * WIDE), BF16),
            pltpu.VMEM((3, DEPTH, ROWS, WIDE), F32),
            pltpu.VMEM((DEPTH, ROWS, WIDE), F32),
            pltpu.VMEM((DEPTH, ROWS, WIDE), F32),
            pltpu.VMEM(block, F32),
            pltpu.VMEM((CELLS, WIDE), F32),
            pltpu.VMEM((slabs, WIDE, group), BF16),
            pltpu.VMEM((slabs, KEYS, group), BF16),
            pltpu.VMEM((2, 8, ROWS, WIDE), F32),
            pltpu.VMEM((24, ROWS, WIDE), F32),
            pltpu.VMEM((slabs, 4, group), F32),
            pltpu.VMEM((slabs, 4, group), F32),
            pltpu.VMEM((slabs, 4, group), F32),
            pltpu.VMEM((slabs, 4, group), F32),
            pltpu.VMEM((2, 1, 128), F32),
            pltpu.VMEM((n_a, 1, 128), F32),
            pltpu.VMEM((n_b, 1, 128), F32),
            dma,
            dma((4,)),
            dma((2,)),
            dma((2,)),
            dma((2,)),
            dma,
            dma((slabs,)),
            dma((2,)),
            dma((2,)),
            pltpu.SemaphoreType.REGULAR,
        ],
        compiler_params=pltpu.CompilerParams(collective_id=0, has_side_effects=True),
        name="render_gradient",
    )(
        voxel_grid,
        first_moment,
        second_moment,
        pixel_index.reshape(1, rays),
        start_slab.reshape(1, rays),
        ray_count.reshape(1, rays),
        target,
    )
    limit = CLIP_RMS * math.sqrt(4.0 * total_depth * total_x * WIDE)
    return pl.pallas_call(
        functools.partial(update_kernel, limit),
        out_shape=[jax.ShapeDtypeStruct(block, F32)] * 3,
        in_specs=[inside] * 5,
        out_specs=[anywhere] * 3,
        scratch_shapes=[held, held, held, dma((3,))],
        compiler_params=pltpu.CompilerParams(vmem_limit_bytes=16 * 2**20),
        name="clipped_adam",
    )(grid, first, second, grad, total)


def solution(mesh):
    torus = Mesh(mesh.devices.reshape(mesh.shape["slab"], 4, 8, 2), AXES)
    cells = P(None, "slab", TILE, None)
    rays = P(TILE)
    return jax.shard_map(
        per_device,
        mesh=torus,
        in_specs=(cells, cells, cells, rays, rays, rays, P(None, TILE)),
        out_specs=(cells, cells, cells),
        check_vma=False,
    )
```

time: 47.5 us -> 39.5 us (0.83)
  Pallas kernels: 46.6 us -> 38.7 us
    pallas_call x1, Pallas kernels: 42.6 us -> 37.2 us  [per_device(): pl.pallas_call(functools.partial(gradient_kernel, sizes, STEP_SPAN / tota...]
    pallas_call x1, Pallas kernels: 3.98 us -> 1.48 us  [per_device(): pl.pallas_call(functools.partial(update_kernel, limit), out_shape=[jax.Sh...]
where the time goes in v2:
time: 39.5 us; the launch traced here: 39.4 us
  Pallas kernels  38.7 us (98%)
  between operations  0.64 us (2%)
    pallas_call x1, Pallas kernels, per_device(): pl.pallas_call(functools.partial(gradient_kernel, sizes, STEP_SPAN / tota...  37.2 us
    pallas_call x1, Pallas kernels, per_device(): pl.pallas_call(functools.partial(update_kernel, limit), out_shape=[jax.Sh...  1.48 us

profile of v2, /device:TPU:1, one launch (start us, length us, event | category | flops | bytes accessed | tf_op | source)
XLA Modules:
  0.0 39.4 jit_solution(1479832034464126837)
XLA Ops:
  0.6 37.2 %render_gradient.1 = (f32[4,16,8,256]{3,2,1,0:T(8,128)S(1)}, f32[4,16,8,256]{3,2,1,0:T(8,128)S(1)}, f32[4,16,8,256]{3,2,1,0:T(8,128)S(1)}, f32[4,16,8,256]{3,2,1,0:T(8,128)S(1)}, f32[1,128]{1,0:T(1,128)S(1)}) custom-call(f32[4,16,8,256]{3,2,1,0:T(8,128)} %grid_hbm.1, f32[4,16,8,256]{3,2,1,0:T(8,128)} %first_hbm.1, f32[4,16,8,256]{3,2,1,0:T(8,128)} %second_hbm.1, ...), custom_call_target="tpu_custom_call" | custom-call | tf_op jit(solution)/shard_map/render_gradient/pallas_call | solution.py:428
  37.9 1.5 %clipped_adam.1 = (f32[4,16,8,256]{3,2,1,0:T(8,128)}, f32[4,16,8,256]{3,2,1,0:T(8,128)}, f32[4,16,8,256]{3,2,1,0:T(8,128)}) custom-call(f32[4,16,8,256]{3,2,1,0:T(8,128)S(1)} %get-tuple-element.8.grid, f32[4,16,8,256]{3,2,1,0:T(8,128)S(1)} %get-tuple-element.9.first, f32[4,16,8,256]{3,2,1,0:T(8,128)S(1)} %get-tuple-element.10.second, ...), custom_call_target="tpu_custom_call" | custom-call | tf_op jit(solution)/shard_map/clipped_adam/pallas_call | solution.py:478

commit v3 on v2

--- a/solution.py
+++ b/solution.py
@@ -69,6 +69,8 @@
     spread,
     columns,
     chosens,
+    rank,
+    rank_half,
     edges,
     halo,
     out_part,
@@ -99,6 +101,10 @@
     tile = (at_x * size_y + at_y) * cores + core
     n_a = slabs * cores
     n_b = size_x * size_y
+    lead = cores - 1
+    leads = core == lead
+    me_a = slab * cores + core
+    me_b = at_x * size_y + at_y
 
     def remote(source, into, send, recv, device):
         return pltpu.make_async_remote_copy(
@@ -128,13 +134,13 @@
     def device_a(off):
         return ((slab + off[0]) % slabs, at_x, at_y, (core + off[1]) % cores)
 
-    def device_b(off):
-        return (slab, (at_x + off[0]) % size_x, (at_y + off[1]) % size_y, core)
+    def device_b(off, at_core):
+        return (slab, (at_x + off[0]) % size_x, (at_y + off[1]) % size_y, at_core)
 
     barrier = pltpu.get_barrier_semaphore()
     greet = [device_a(off) for off in over_a]
-    greet += [device_b((0, y)) for y in far_first(size_y)]
-    greet += [device_b((x, 0)) for x in far_first(size_x)]
+    greet += [device_b((0, y), core) for y in far_first(size_y)]
+    greet += [device_b((x, 0), core) for x in far_first(size_x)]
     next_tile = tile_device((tile + 1) % tiles)
     prev_tile = tile_device((tile + tiles - 1) % tiles)
     greet += [next_tile, prev_tile]
@@ -157,6 +163,12 @@
     ]
     for load in moment_loads:
         load.start()
+
+    row_at = lax.broadcasted_iota(jnp.int32, (ROWS, WIDE), 0)
+    lane_at = lax.broadcasted_iota(jnp.int32, (ROWS, WIDE), 1)
+    rank[...] = lax.broadcasted_iota(jnp.int32, (KEYS, 128), 0)
+    rank_half[...] = lax.broadcasted_iota(jnp.int32, (WIDE, 128), 0).astype(F32).astype(BF16)
+    spread[...] = jnp.zeros_like(spread)
 
     load_grid.wait()
     light = jnp.ones((ROWS, WIDE), F32)
@@ -188,8 +200,11 @@
         half = (place + 1) // 2
         return (slab + half * (2 * (place % 2) - 1) + slabs) % slabs
 
-    def ring(other):
-        return (other, at_x, at_y, core)
+    def leader(other):
+        return (other, at_x, at_y, lead)
+
+    def packed_row(row):
+        return jnp.broadcast_to(row.astype(F32), (16, group)).astype(BF16)
 
     def look_up(other):
         lanes = pl.ds(pl.multiple_of(other * group, group), group)
@@ -197,31 +212,43 @@
         begin = start[:, lanes]
         taken = begin * DEPTH + count[:, lanes] - slab * DEPTH
         taken = jnp.where(begin <= slab, jnp.clip(taken, 0, DEPTH), 0)
-        key = (taken - 1) * ROWS + cell // WIDE
-        across = lax.broadcasted_iota(jnp.int32, (WIDE, group), 0)
-        column = jnp.where(across == cell % WIDE, 1.0, 0.0).astype(BF16)
-        columns[other] = column
-        found = jnp.dot(
-            table[...],
-            jnp.concatenate([column, column], axis=0),
-            preferred_element_type=F32,
-        )
-        chosen = lax.broadcasted_iota(jnp.int32, (KEYS, group), 0) == key
-        chosens[other] = jnp.where(chosen, 1.0, 0.0).astype(BF16)
-        values = [
-            jnp.sum(
-                jnp.where(chosen, found[c * KEYS : (c + 1) * KEYS], 0.0),
-                axis=0,
-                keepdims=True,
+        key = (taken - 1) * ROWS + lax.shift_right_logical(cell, 8)
+        one = jnp.ones((16, 128), BF16)
+        zero = jnp.zeros((16, 128), BF16)
+        for ref, row, height in (
+            (columns, packed_row(cell & (WIDE - 1)), WIDE),
+            (chosens, packed_row(key), KEYS),
+        ):
+            for k in range(0, height, 16):
+                level = rank_half[pl.ds(k, 16), :]
+                for t in range(0, group, 128):
+                    ref[other, pl.ds(k, 16), pl.ds(t, 128)] = jnp.where(
+                        level == row[:, t : t + 128], one, zero
+                    )
+        rows = []
+        for half in range(0, group, WIDE):
+            column = columns[other, :, pl.ds(half, WIDE)]
+            found = jnp.dot(
+                table[...],
+                jnp.concatenate([column, column], axis=0),
+                preferred_element_type=F32,
             )
-            for c in range(4)
-        ]
+            for t in range(0, WIDE, 128):
+                wanted = jnp.broadcast_to(key[:, half + t : half + t + 128], (ROWS, 128))
+                kept = [jnp.zeros((ROWS, 128), F32) for _ in range(4)]
+                for k in range(0, KEYS, ROWS):
+                    hit = rank[pl.ds(k, ROWS), :] == wanted
+                    for c in range(4):
+                        piece = found[c * KEYS + k : c * KEYS + k + ROWS, t : t + 128]
+                        kept[c] = jnp.where(hit, piece, kept[c])
+                rows.append([jnp.sum(keep, axis=0, keepdims=True) for keep in kept])
+        values = [jnp.concatenate([row[c] for row in rows], axis=1) for c in range(4)]
         values[3] = 1.0 - values[3]
         return jnp.concatenate(values, axis=0)
 
-    def send_part(other):
+    def send_part(slot, into, other):
         remote(
-            out_part.at[other], in_part.at[slab], part_sem.at[0], part_sem.at[1], ring(other)
+            out_part.at[slot], in_part.at[into], part_sem.at[0], part_sem.at[1], leader(other)
         ).start()
 
     places = list(range(slabs - 1, 0, -1))
@@ -230,14 +257,19 @@
         out_part[partner(place)] = look_up(partner(place))
     pl.semaphore_wait(barrier, len(greet))
     for place in early:
-        send_part(partner(place))
+        send_part(partner(place), me_a, partner(place))
     for place in places[slabs // 2 :]:
         out_part[partner(place)] = look_up(partner(place))
-        send_part(partner(place))
-    in_part[slab] = look_up(slab)
-
-    for off in far_first(size_y):
-        signal(ready, device_b((0, off)))
+        send_part(partner(place), me_a, partner(place))
+    out_part[slab] = look_up(slab)
+    goal = target[:, pl.ds(pl.multiple_of(slab * group, group), group)]
+
+    @pl.when(jnp.logical_not(leads))
+    def _():
+        send_part(slab, me_a, slab)
+        out_part[slabs] = jnp.concatenate([goal, jnp.zeros((1, group), F32)], axis=0)
+        send_part(slabs, n_a, slab)
+
     for c in range(4):
         for z in range(DEPTH):
             k = c * DEPTH + z
@@ -251,34 +283,54 @@
     ):
         remote(source, into, halo_sem.at[0], halo_sem.at[1], device).start()
 
-    others = pl.ds(0, slabs - 1)
-    all_parts = remote(
-        out_part.at[others], in_part.at[others], part_sem.at[0], part_sem.at[1], ring(slab)
-    )
-    goal = target[:, pl.ds(pl.multiple_of(slab * group, group), group)]
-    all_parts.wait_recv()
-    ahead = jnp.ones((1, group), F32)
-    rendered = jnp.zeros((3, group), F32)
-    reach = []
-    for s in range(slabs):
-        reach.append(ahead)
-        part = in_part[s]
-        rendered = rendered + ahead * part[:3]
-        ahead = ahead * part[3:]
-    residual = RENDER_WEIGHT * (rendered + ahead * BACKGROUND - goal)
-    beyond = jnp.full((3, group), BACKGROUND, F32)
-    for s in range(slabs - 1, -1, -1):
-        product = residual * beyond
-        dark = product[0:1] + product[1:2] + product[2:3]
-        out_cot[s] = reach[s] * jnp.concatenate([residual, dark], axis=0)
-        part = in_part[s]
-        beyond = part[:3] + part[3:] * beyond
-
-    for place in places:
-        other = partner(place)
-        remote(
-            out_cot.at[other], in_cot.at[slab], cot_send, cot_recv.at[slab], ring(other)
-        ).start()
+    def part_blocks(n):
+        part = in_part.at[pl.ds(0, n)]
+        return remote(part, part, part_sem.at[0], part_sem.at[1], next_tile)
+
+    def cot_blocks(n, slot):
+        cot = out_cot.at[pl.ds(0, n)]
+        return remote(cot, cot, cot_send, cot_recv.at[slot], next_tile)
+
+    @pl.when(leads)
+    def _():
+        for x in far_first(size_x):
+            signal(ready.at[0], device_b((x, 0), lead))
+        in_part[me_a] = out_part[slab]
+        part_blocks(n_a).wait_recv()
+        for c in range(cores):
+            ahead = jnp.ones((1, group), F32)
+            rendered = jnp.zeros((3, group), F32)
+            reach = []
+            for s in range(slabs):
+                reach.append(ahead)
+                part = in_part[s * cores + c]
+                rendered = rendered + ahead * part[:3]
+                ahead = ahead * part[3:]
+            wish = goal if c == lead else in_part[n_a][:3]
+            residual = RENDER_WEIGHT * (rendered + ahead * BACKGROUND - wish)
+            beyond = jnp.full((3, group), BACKGROUND, F32)
+            for s in range(slabs - 1, -1, -1):
+                product = residual * beyond
+                dark = product[0:1] + product[1:2] + product[2:3]
+                out_cot[s * cores + c] = reach[s] * jnp.concatenate([residual, dark], axis=0)
+                part = in_part[s * cores + c]
+                beyond = part[:3] + part[3:] * beyond
+        for place in places + [0]:
+            other = partner(place)
+            for c in range(cores):
+                if place or c != lead:
+                    remote(
+                        out_cot.at[other * cores + c],
+                        in_cot.at[slab],
+                        cot_send,
+                        cot_recv.at[slab],
+                        (other, at_x, at_y, c),
+                    ).start()
+        in_cot[slab] = out_cot[slab * cores + lead]
+        if size_x > 1:
+            pl.semaphore_wait(ready.at[0], size_x - 1)
+        for y in far_first(size_y):
+            signal(ready.at[1], device_b((0, y), lead))
 
     def scatter(other, cot):
         high, low = split_bf16(cot)
@@ -298,11 +350,7 @@
             preferred_element_type=F32,
         )
 
-    spread[...] = scatter(slab, out_cot[slab])
-
     remote(halo, halo, halo_sem.at[0], halo_sem.at[1], next_tile).wait()
-    row_at = lax.broadcasted_iota(jnp.int32, (ROWS, WIDE), 0)
-    lane_at = lax.broadcasted_iota(jnp.int32, (ROWS, WIDE), 1)
 
     def smooth_channel(c, carry):
         for z in range(DEPTH):
@@ -335,13 +383,15 @@
 
     def scatter_arrived(place, carry):
         other = partner(place)
-        remote(
-            out_cot.at[other], in_cot.at[other], cot_send, cot_recv.at[other], ring(other)
-        ).wait_recv()
+
+        @pl.when((place > 0) | jnp.logical_not(leads))
+        def _():
+            cot_blocks(1, other).wait_recv()
+
         spread[...] += scatter(other, in_cot[other])
         return carry
 
-    lax.fori_loop(1, slabs, scatter_arrived, 0)
+    lax.fori_loop(0, slabs, scatter_arrived, 0)
 
     later = [jnp.zeros((ROWS, WIDE), F32) for _ in range(3)]
     tail = jnp.zeros((ROWS, WIDE), F32)
@@ -367,28 +417,54 @@
     squares = squares[:, :128] + squares[:, 128:]
     own = jnp.sum(squares, axis=0, keepdims=True)
     mine[0] = own
-    me_a = slab * cores + core
-    for off in over_a:
-        remote(mine.at[0], sums_a.at[me_a], a_sem.at[0], a_sem.at[1], device_a(off)).start()
-    sums_a[me_a] = own
-    all_parts.wait_send()
-    remote(
-        out_cot.at[others], in_cot.at[others], cot_send, cot_recv.at[0], ring(slab)
-    ).wait_send()
-    for load in moment_loads:
-        load.wait()
-    if size_y > 1:
-        pl.semaphore_wait(ready, size_y - 1)
-    some = sums_a.at[pl.ds(0, n_a - 1)]
-    remote(some, some, a_sem.at[0], a_sem.at[1], next_tile).wait()
-    own = jnp.sum(sums_a[...], axis=0)
-    mine[1] = own
-    me_b = at_x * size_y + at_y
-    for off in over_b:
-        remote(mine.at[1], sums_b.at[me_b], b_sem.at[0], b_sem.at[1], device_b(off)).start()
-    sums_b[me_b] = own
-    some = sums_b.at[pl.ds(0, n_b - 1)]
-    remote(some, some, b_sem.at[0], b_sem.at[1], next_tile).wait()
+
+    def send_a(other):
+        remote(mine.at[0], sums_a.at[me_a], a_sem.at[0], a_sem.at[1], leader(other)).start()
+
+    def blocks(sums, n, send, recv):
+        some = sums.at[pl.ds(0, n)]
+        return remote(some, some, send, recv, next_tile)
+
+    for off in far_first(slabs):
+        send_a((slab + off) % slabs)
+
+    @pl.when(jnp.logical_not(leads))
+    def _():
+        send_a(slab)
+        part_blocks(slabs + 1).wait_send()
+        blocks(sums_a, slabs, a_sem.at[0], a_sem.at[1]).wait_send()
+        for load in moment_loads:
+            load.wait()
+        blocks(sums_b, n_b, b_sem.at[0], b_sem.at[2]).wait_recv()
+
+    @pl.when(leads)
+    def _():
+        sums_a[me_a] = own
+        part_blocks(slabs - 1).wait_send()
+        cot_blocks(n_a - 1, 0).wait_send()
+        for load in moment_loads:
+            load.wait()
+        if size_y > 1:
+            pl.semaphore_wait(ready.at[1], size_y - 1)
+        blocks(sums_a, n_a - 1, a_sem.at[0], a_sem.at[1]).wait_recv()
+        share_b = jnp.sum(sums_a[...], axis=0)
+        mine[1] = share_b
+        for off in over_b + [(0, 0)]:
+            for c in range(cores):
+                if off != (0, 0) or c != lead:
+                    remote(
+                        mine.at[1],
+                        sums_b.at[me_b],
+                        b_sem.at[1 if c == lead else 0],
+                        b_sem.at[2],
+                        device_b(off, c),
+                    ).start()
+        sums_b[me_b] = share_b
+        blocks(sums_a, slabs - 1, a_sem.at[0], a_sem.at[1]).wait_send()
+        blocks(sums_b, n_b, b_sem.at[0], b_sem.at[2]).wait_send()
+        if n_b > 1:
+            blocks(sums_b, n_b - 1, b_sem.at[1], b_sem.at[2]).wait()
+
     total_ref[...] = jnp.sum(sums_b[...], axis=0)
 
 
@@ -443,11 +519,13 @@
             pltpu.VMEM((CELLS, WIDE), F32),
             pltpu.VMEM((slabs, WIDE, group), BF16),
             pltpu.VMEM((slabs, KEYS, group), BF16),
+            pltpu.VMEM((KEYS, 128), jnp.int32),
+            pltpu.VMEM((WIDE, 128), BF16),
             pltpu.VMEM((2, 8, ROWS, WIDE), F32),
             pltpu.VMEM((24, ROWS, WIDE), F32),
-            pltpu.VMEM((slabs, 4, group), F32),
-            pltpu.VMEM((slabs, 4, group), F32),
-            pltpu.VMEM((slabs, 4, group), F32),
+            pltpu.VMEM((slabs + 1, 4, group), F32),
+            pltpu.VMEM((n_a + 1, 4, group), F32),
+            pltpu.VMEM((n_a, 4, group), F32),
             pltpu.VMEM((slabs, 4, group), F32),
             pltpu.VMEM((2, 1, 128), F32),
             pltpu.VMEM((n_a, 1, 128), F32),
@@ -460,8 +538,8 @@
             dma,
             dma((slabs,)),
             dma((2,)),
-            dma((2,)),
-            pltpu.SemaphoreType.REGULAR,
+            dma((3,)),
+            pltpu.SemaphoreType.REGULAR((2,)),
         ],
         compiler_params=pltpu.CompilerParams(collective_id=0, has_side_effects=True),
         name="render_gradient",

time: 39.5 us -> 39.3 us (level)
  no operation moved by 1% of the time
where the time goes in v3:
time: 39.3 us; the launch traced here: 39.2 us
  Pallas kernels  38.6 us (98%)
  between operations  0.64 us (2%)
    pallas_call x1, Pallas kernels, per_device(): pl.pallas_call(functools.partial(gradient_kernel, sizes, STEP_SPAN / tota...  37.1 us
    pallas_call x1, Pallas kernels, per_device(): pl.pallas_call(functools.partial(update_kernel, limit), out_shape=[jax.Sh...  1.48 us

profile of v3, /device:TPU:1, one launch (start us, length us, event | category | flops | bytes accessed | tf_op | source)
XLA Modules:
  0.0 39.2 jit_solution(45283706651951310)
XLA Ops:
  0.6 37.1 %render_gradient.1 = (f32[4,16,8,256]{3,2,1,0:T(8,128)S(1)}, f32[4,16,8,256]{3,2,1,0:T(8,128)S(1)}, f32[4,16,8,256]{3,2,1,0:T(8,128)S(1)}, f32[4,16,8,256]{3,2,1,0:T(8,128)S(1)}, f32[1,128]{1,0:T(1,128)S(1)}) custom-call(f32[4,16,8,256]{3,2,1,0:T(8,128)} %grid_hbm.1, f32[4,16,8,256]{3,2,1,0:T(8,128)} %first_hbm.1, f32[4,16,8,256]{3,2,1,0:T(8,128)} %second_hbm.1, ...), custom_call_target="tpu_custom_call" | custom-call | tf_op jit(solution)/shard_map/render_gradient/pallas_call | solution.py:504
  37.7 1.5 %clipped_adam.1 = (f32[4,16,8,256]{3,2,1,0:T(8,128)}, f32[4,16,8,256]{3,2,1,0:T(8,128)}, f32[4,16,8,256]{3,2,1,0:T(8,128)}) custom-call(f32[4,16,8,256]{3,2,1,0:T(8,128)S(1)} %get-tuple-element.8.grid, f32[4,16,8,256]{3,2,1,0:T(8,128)S(1)} %get-tuple-element.9.first, f32[4,16,8,256]{3,2,1,0:T(8,128)S(1)} %get-tuple-element.10.second, ...), custom_call_target="tpu_custom_call" | custom-call | tf_op jit(solution)/shard_map/clipped_adam/pallas_call | solution.py:556

commit v4 on v3

--- a/solution.py
+++ b/solution.py
@@ -68,6 +68,7 @@
     smooth,
     spread,
     columns,
+    upright,
     chosens,
     rank,
     rank_half,
@@ -190,9 +191,9 @@
         if z % 2:
             for c in range(4):
                 high, low = split_bf16(jnp.concatenate([pairs[-2][c], pairs[-1][c]], axis=0))
-                rows = pl.ds(c * KEYS + (z - 1) * ROWS, 2 * ROWS)
-                table[rows, pl.ds(0, WIDE)] = high
-                table[rows, pl.ds(WIDE, WIDE)] = low
+                at = c * KEYS + (z - 1) * ROWS
+                table[pl.ds(at, 2 * ROWS), :] = high
+                table[pl.ds(CELLS + at, 2 * ROWS), :] = low
     for load in ray_loads:
         load.wait()
 
@@ -227,11 +228,8 @@
                     )
         rows = []
         for half in range(0, group, WIDE):
-            column = columns[other, :, pl.ds(half, WIDE)]
             found = jnp.dot(
-                table[...],
-                jnp.concatenate([column, column], axis=0),
-                preferred_element_type=F32,
+                table[...], columns[other, :, pl.ds(half, WIDE)], preferred_element_type=F32
             )
             for t in range(0, WIDE, 128):
                 wanted = jnp.broadcast_to(key[:, half + t : half + t + 128], (ROWS, 128))
@@ -239,8 +237,11 @@
                 for k in range(0, KEYS, ROWS):
                     hit = rank[pl.ds(k, ROWS), :] == wanted
                     for c in range(4):
-                        piece = found[c * KEYS + k : c * KEYS + k + ROWS, t : t + 128]
-                        kept[c] = jnp.where(hit, piece, kept[c])
+                        high, low = (
+                            found[at + c * KEYS + k : at + c * KEYS + k + ROWS, t : t + 128]
+                            for at in (0, CELLS)
+                        )
+                        kept[c] = jnp.where(hit, high + low, kept[c])
                 rows.append([jnp.sum(keep, axis=0, keepdims=True) for keep in kept])
         values = [jnp.concatenate([row[c] for row in rows], axis=1) for c in range(4)]
         values[3] = 1.0 - values[3]
@@ -282,6 +283,23 @@
         (grid.at[:, 0], halo.at[pl.ds(4, 4)], device_a((slabs - 1, 0))),
     ):
         remote(source, into, halo_sem.at[0], halo_sem.at[1], device).start()
+
+    def stand_up(other, carry):
+        cell = pixel[:, pl.ds(pl.multiple_of(other * group, group), group)]
+        column = (cell & (WIDE - 1)).astype(F32)
+        level = lax.broadcasted_iota(jnp.int32, (16, WIDE), 1).astype(F32).astype(BF16)
+        one = jnp.ones((16, WIDE), BF16)
+        zero = jnp.zeros((16, WIDE), BF16)
+        for t in range(0, group, 128):
+            down = jnp.broadcast_to(column[:, t : t + 128], (128, 128)).T.astype(BF16)
+            for k in range(0, 128, 16):
+                tall = down[k : k + 16]
+                upright[other, pl.ds(t + k, 16), :] = jnp.where(
+                    jnp.concatenate([tall] * (WIDE // 128), axis=1) == level, one, zero
+                )
+        return carry
+
+    lax.fori_loop(0, slabs, stand_up, 0)
 
     def part_blocks(n):
         part = in_part.at[pl.ds(0, n)]
@@ -315,7 +333,7 @@
                 out_cot[s * cores + c] = reach[s] * jnp.concatenate([residual, dark], axis=0)
                 part = in_part[s * cores + c]
                 beyond = part[:3] + part[3:] * beyond
-        for place in places + [0]:
+        for place in range(slabs):
             other = partner(place)
             for c in range(cores):
                 if place or c != lead:
@@ -335,20 +353,11 @@
     def scatter(other, cot):
         high, low = split_bf16(cot)
         chosen = chosens[other]
-        column = columns[other]
         left = jnp.concatenate(
-            [
-                jnp.concatenate([chosen * high[c : c + 1], chosen * low[c : c + 1]], axis=1)
-                for c in range(4)
-            ],
-            axis=0,
+            [chosen * half[c : c + 1] for half in (high, low) for c in range(4)], axis=0
         )
-        return lax.dot_general(
-            left,
-            jnp.concatenate([column, column], axis=1),
-            (((1,), (1,)), ((), ())),
-            preferred_element_type=F32,
-        )
+        found = jnp.dot(left, upright[other], preferred_element_type=F32)
+        return found[:CELLS] + found[CELLS:]
 
     remote(halo, halo, halo_sem.at[0], halo_sem.at[1], next_tile).wait()
 
@@ -511,13 +520,14 @@
             pltpu.VMEM((1, rays), jnp.int32),
             pltpu.VMEM((1, rays), jnp.int32),
             pltpu.VMEM((3, rays), F32),
-            pltpu.VMEM((CELLS, 2 * WIDE), BF16),
+            pltpu.VMEM((2 * CELLS, WIDE), BF16),
             pltpu.VMEM((3, DEPTH, ROWS, WIDE), F32),
             pltpu.VMEM((DEPTH, ROWS, WIDE), F32),
             pltpu.VMEM((DEPTH, ROWS, WIDE), F32),
             pltpu.VMEM(block, F32),
             pltpu.VMEM((CELLS, WIDE), F32),
             pltpu.VMEM((slabs, WIDE, group), BF16),
+            pltpu.VMEM((slabs, group, WIDE), BF16),
             pltpu.VMEM((slabs, KEYS, group), BF16),
             pltpu.VMEM((KEYS, 128), jnp.int32),
             pltpu.VMEM((WIDE, 128), BF16),

time: 39.3 us -> 38.7 us (0.985)
  Pallas kernels: 38.6 us -> 38 us
    pallas_call x1, Pallas kernels: 37.1 us -> 36.5 us  [per_device(): pl.pallas_call(functools.partial(gradient_kernel, sizes, STEP_SPAN / tota...]
where the time goes in v4:
time: 38.7 us; the launch traced here: 38.6 us
  Pallas kernels  38 us (98%)
  between operations  0.64 us (2%)
    pallas_call x1, Pallas kernels, per_device(): pl.pallas_call(functools.partial(gradient_kernel, sizes, STEP_SPAN / tota...  36.5 us
    pallas_call x1, Pallas kernels, per_device(): pl.pallas_call(functools.partial(update_kernel, limit), out_shape=[jax.Sh...  1.48 us

profile of v4, /device:TPU:1, one launch (start us, length us, event | category | flops | bytes accessed | tf_op | source)
XLA Modules:
  0.0 38.6 jit_solution(18444640409343076744)
XLA Ops:
  0.6 36.5 %render_gradient.1 = (f32[4,16,8,256]{3,2,1,0:T(8,128)S(1)}, f32[4,16,8,256]{3,2,1,0:T(8,128)S(1)}, f32[4,16,8,256]{3,2,1,0:T(8,128)S(1)}, f32[4,16,8,256]{3,2,1,0:T(8,128)S(1)}, f32[1,128]{1,0:T(1,128)S(1)}) custom-call(f32[4,16,8,256]{3,2,1,0:T(8,128)} %grid_hbm.1, f32[4,16,8,256]{3,2,1,0:T(8,128)} %first_hbm.1, f32[4,16,8,256]{3,2,1,0:T(8,128)} %second_hbm.1, ...), custom_call_target="tpu_custom_call" | custom-call | tf_op jit(solution)/shard_map/render_gradient/pallas_call | solution.py:513
  37.1 1.5 %clipped_adam.1 = (f32[4,16,8,256]{3,2,1,0:T(8,128)}, f32[4,16,8,256]{3,2,1,0:T(8,128)}, f32[4,16,8,256]{3,2,1,0:T(8,128)}) custom-call(f32[4,16,8,256]{3,2,1,0:T(8,128)S(1)} %get-tuple-element.8.grid, f32[4,16,8,256]{3,2,1,0:T(8,128)S(1)} %get-tuple-element.9.first, f32[4,16,8,256]{3,2,1,0:T(8,128)S(1)} %get-tuple-element.10.second, ...), custom_call_target="tpu_custom_call" | custom-call | tf_op jit(solution)/shard_map/clipped_adam/pallas_call | solution.py:566

commit v5 on v4

--- a/solution.py
+++ b/solution.py
@@ -140,7 +140,14 @@
 
     barrier = pltpu.get_barrier_semaphore()
     greet = [device_a(off) for off in over_a]
-    greet += [device_b((0, y), core) for y in far_first(size_y)]
+    assert size_y <= 8
+    two_away = [y for y in far_first(size_y) if min(y, size_y - y) == 2] if size_y > 4 else []
+    greet += [
+        device_b((0, y), c)
+        for y in far_first(size_y)
+        if min(y, size_y - y) <= 2
+        for c in range(cores)
+    ]
     greet += [device_b((x, 0), core) for x in far_first(size_x)]
     next_tile = tile_device((tile + 1) % tiles)
     prev_tile = tile_device((tile + tiles - 1) % tiles)
@@ -162,16 +169,15 @@
         pltpu.make_async_copy(first_hbm, first, moment_sem.at[0]),
         pltpu.make_async_copy(second_hbm, second, moment_sem.at[1]),
     ]
-    for load in moment_loads:
-        load.start()
 
     row_at = lax.broadcasted_iota(jnp.int32, (ROWS, WIDE), 0)
     lane_at = lax.broadcasted_iota(jnp.int32, (ROWS, WIDE), 1)
     rank[...] = lax.broadcasted_iota(jnp.int32, (KEYS, 128), 0)
     rank_half[...] = lax.broadcasted_iota(jnp.int32, (WIDE, 128), 0).astype(F32).astype(BF16)
-    spread[...] = jnp.zeros_like(spread)
 
     load_grid.wait()
+    for load in moment_loads:
+        load.start()
     light = jnp.ones((ROWS, WIDE), F32)
     color = [jnp.zeros((ROWS, WIDE), F32) for _ in range(3)]
     pairs = []
@@ -311,8 +317,8 @@
 
     @pl.when(leads)
     def _():
-        for x in far_first(size_x):
-            signal(ready.at[0], device_b((x, 0), lead))
+        for y in two_away:
+            signal(ready.at[0], device_b((0, y), lead))
         in_part[me_a] = out_part[slab]
         part_blocks(n_a).wait_recv()
         for c in range(cores):
@@ -345,19 +351,31 @@
                         (other, at_x, at_y, c),
                     ).start()
         in_cot[slab] = out_cot[slab * cores + lead]
-        if size_x > 1:
-            pl.semaphore_wait(ready.at[0], size_x - 1)
-        for y in far_first(size_y):
-            signal(ready.at[1], device_b((0, y), lead))
-
-    def scatter(other, cot):
-        high, low = split_bf16(cot)
-        chosen = chosens[other]
-        left = jnp.concatenate(
-            [chosen * half[c : c + 1] for half in (high, low) for c in range(4)], axis=0
-        )
-        found = jnp.dot(left, upright[other], preferred_element_type=F32)
-        return found[:CELLS] + found[CELLS:]
+        if two_away:
+            pl.semaphore_wait(ready.at[0], len(two_away))
+        for x in far_first(size_x):
+            signal(ready.at[1], device_b((x, 0), lead))
+
+    def scatter(others):
+        right = jnp.concatenate([upright[other] for other in others], axis=0)
+        halves = [split_bf16(in_cot[other]) for other in others]
+        found = [
+            jnp.dot(
+                jnp.concatenate(
+                    [
+                        jnp.concatenate(
+                            [chosens[other] * half[part][c : c + 1] for c in range(4)], axis=0
+                        )
+                        for other, half in zip(others, halves)
+                    ],
+                    axis=1,
+                ),
+                right,
+                preferred_element_type=F32,
+            )
+            for part in (0, 1)
+        ]
+        return found[0] + found[1]
 
     remote(halo, halo, halo_sem.at[0], halo_sem.at[1], next_tile).wait()
 
@@ -390,17 +408,17 @@
 
     lax.fori_loop(0, 4, smooth_channel, 0)
 
-    def scatter_arrived(place, carry):
-        other = partner(place)
-
-        @pl.when((place > 0) | jnp.logical_not(leads))
-        def _():
+    @pl.when(jnp.logical_not(leads))
+    def _():
+        cot_blocks(1, slab).wait_recv()
+
+    spread[...] = scatter([slab])
+    for first_place, past in ((1, 3), (3, 5), (5, 8)):
+        arrived = [partner(place) for place in range(first_place, min(past, slabs))]
+        for other in arrived:
             cot_blocks(1, other).wait_recv()
-
-        spread[...] += scatter(other, in_cot[other])
-        return carry
-
-    lax.fori_loop(0, slabs, scatter_arrived, 0)
+        if arrived:
+            spread[...] += scatter(arrived)
 
     later = [jnp.zeros((ROWS, WIDE), F32) for _ in range(3)]
     tail = jnp.zeros((ROWS, WIDE), F32)
@@ -453,8 +471,8 @@
         cot_blocks(n_a - 1, 0).wait_send()
         for load in moment_loads:
             load.wait()
-        if size_y > 1:
-            pl.semaphore_wait(ready.at[1], size_y - 1)
+        if size_x > 1:
+            pl.semaphore_wait(ready.at[1], size_x - 1)
         blocks(sums_a, n_a - 1, a_sem.at[0], a_sem.at[1]).wait_recv()
         share_b = jnp.sum(sums_a[...], axis=0)
         mine[1] = share_b
@@ -480,16 +498,18 @@
 def update_kernel(limit, grid, first, second, grad, total, *rest):
     outs, held, sem = rest[:3], rest[3:6], rest[6]
     norm = jnp.sqrt(jnp.sum(total[...], axis=1, keepdims=True))
-    scale = limit / jnp.maximum(norm, limit)
+    scale = jnp.broadcast_to(limit / jnp.maximum(norm, limit), (ROWS, WIDE))
+    rate = LEARN_RATE / (1.0 - BETA_ONE**STEP)
     for c in range(4):
-        clipped = grad[c] * scale
-        new_first = BETA_ONE * first[c] + (1.0 - BETA_ONE) * clipped
-        new_second = BETA_TWO * second[c] + (1.0 - BETA_TWO) * clipped * clipped
-        held[1][c] = new_first
-        held[2][c] = new_second
-        first_hat = new_first * (1.0 / (1.0 - BETA_ONE**STEP))
-        second_hat = new_second * (1.0 / (1.0 - BETA_TWO**STEP))
-        held[0][c] = grid[c] - LEARN_RATE * first_hat / (jnp.sqrt(second_hat) + EPSILON)
+        for z in range(DEPTH):
+            clipped = grad[c, z] * scale
+            new_first = BETA_ONE * first[c, z] + (1.0 - BETA_ONE) * clipped
+            new_second = BETA_TWO * second[c, z] + ((1.0 - BETA_TWO) * clipped) * clipped
+            second_hat = new_second * (1.0 / (1.0 - BETA_TWO**STEP))
+            root = second_hat * lax.rsqrt(second_hat)
+            held[0][c, z] = grid[c, z] - (rate * new_first) * pl.reciprocal(root + EPSILON)
+            held[1][c, z] = new_first
+            held[2][c, z] = new_second
         for k in range(3):
             pltpu.make_async_copy(held[k].at[c], outs[k].at[c], sem.at[k]).start()
     for k in range(3):

time: 38.7 us -> 40.8 us (1.054)
  Pallas kernels: 38 us -> 40 us
    pallas_call x1, Pallas kernels: 36.5 us -> 38.7 us  [per_device(): pl.pallas_call(functools.partial(gradient_kernel, sizes, STEP_SPAN / tota...]
where the time goes in v5:
time: 40.8 us; the launch traced here: 40.7 us
  Pallas kernels  40 us (98%)
  between operations  0.64 us (2%)
    pallas_call x1, Pallas kernels, per_device(): pl.pallas_call(functools.partial(gradient_kernel, sizes, STEP_SPAN / tota...  38.7 us
    pallas_call x1, Pallas kernels, per_device(): pl.pallas_call(functools.partial(update_kernel, limit), out_shape=[jax.Sh...  1.33 us

profile of v5, /device:TPU:1, one launch (start us, length us, event | category | flops | bytes accessed | tf_op | source)
XLA Modules:
  0.0 40.7 jit_solution(13067639017706997957)
XLA Ops:
  0.6 38.7 %render_gradient.1 = (f32[4,16,8,256]{3,2,1,0:T(8,128)S(1)}, f32[4,16,8,256]{3,2,1,0:T(8,128)S(1)}, f32[4,16,8,256]{3,2,1,0:T(8,128)S(1)}, f32[4,16,8,256]{3,2,1,0:T(8,128)S(1)}, f32[1,128]{1,0:T(1,128)S(1)}) custom-call(f32[4,16,8,256]{3,2,1,0:T(8,128)} %grid_hbm.1, f32[4,16,8,256]{3,2,1,0:T(8,128)} %first_hbm.1, f32[4,16,8,256]{3,2,1,0:T(8,128)} %second_hbm.1, ...), custom_call_target="tpu_custom_call" | custom-call | tf_op jit(solution)/shard_map/render_gradient/pallas_call | solution.py:533
  39.4 1.3 %clipped_adam.1 = (f32[4,16,8,256]{3,2,1,0:T(8,128)}, f32[4,16,8,256]{3,2,1,0:T(8,128)}, f32[4,16,8,256]{3,2,1,0:T(8,128)}) custom-call(f32[4,16,8,256]{3,2,1,0:T(8,128)S(1)} %get-tuple-element.8.grid, f32[4,16,8,256]{3,2,1,0:T(8,128)S(1)} %get-tuple-element.9.first, f32[4,16,8,256]{3,2,1,0:T(8,128)S(1)} %get-tuple-element.10.second, ...), custom_call_target="tpu_custom_call" | custom-call | tf_op jit(solution)/shard_map/clipped_adam/pallas_call | solution.py:586

commit v6 on v5

--- a/solution.py
+++ b/solution.py
@@ -175,6 +175,8 @@
     rank[...] = lax.broadcasted_iota(jnp.int32, (KEYS, 128), 0)
     rank_half[...] = lax.broadcasted_iota(jnp.int32, (WIDE, 128), 0).astype(F32).astype(BF16)
 
+    spread[...] = jnp.zeros_like(spread)
+
     load_grid.wait()
     for load in moment_loads:
         load.start()
@@ -265,6 +267,12 @@
     pl.semaphore_wait(barrier, len(greet))
     for place in early:
         send_part(partner(place), me_a, partner(place))
+
+    @pl.when(leads)
+    def _():
+        for y in two_away:
+            signal(ready.at[0], device_b((0, y), lead))
+
     for place in places[slabs // 2 :]:
         out_part[partner(place)] = look_up(partner(place))
         send_part(partner(place), me_a, partner(place))
@@ -317,8 +325,6 @@
 
     @pl.when(leads)
     def _():
-        for y in two_away:
-            signal(ready.at[0], device_b((0, y), lead))
         in_part[me_a] = out_part[slab]
         part_blocks(n_a).wait_recv()
         for c in range(cores):
@@ -351,31 +357,15 @@
                         (other, at_x, at_y, c),
                     ).start()
         in_cot[slab] = out_cot[slab * cores + lead]
-        if two_away:
-            pl.semaphore_wait(ready.at[0], len(two_away))
-        for x in far_first(size_x):
-            signal(ready.at[1], device_b((x, 0), lead))
-
-    def scatter(others):
-        right = jnp.concatenate([upright[other] for other in others], axis=0)
-        halves = [split_bf16(in_cot[other]) for other in others]
-        found = [
-            jnp.dot(
-                jnp.concatenate(
-                    [
-                        jnp.concatenate(
-                            [chosens[other] * half[part][c : c + 1] for c in range(4)], axis=0
-                        )
-                        for other, half in zip(others, halves)
-                    ],
-                    axis=1,
-                ),
-                right,
-                preferred_element_type=F32,
-            )
-            for part in (0, 1)
-        ]
-        return found[0] + found[1]
+
+    def scatter(other):
+        high, low = split_bf16(in_cot[other])
+        chosen = chosens[other]
+        left = jnp.concatenate(
+            [chosen * half[c : c + 1] for half in (high, low) for c in range(4)], axis=0
+        )
+        found = jnp.dot(left, upright[other], preferred_element_type=F32)
+        return found[:CELLS] + found[CELLS:]
 
     remote(halo, halo, halo_sem.at[0], halo_sem.at[1], next_tile).wait()
 
@@ -408,17 +398,25 @@
 
     lax.fori_loop(0, 4, smooth_channel, 0)
 
-    @pl.when(jnp.logical_not(leads))
+    @pl.when(leads)
     def _():
-        cot_blocks(1, slab).wait_recv()
-
-    spread[...] = scatter([slab])
-    for first_place, past in ((1, 3), (3, 5), (5, 8)):
-        arrived = [partner(place) for place in range(first_place, min(past, slabs))]
-        for other in arrived:
+        if two_away:
+            pl.semaphore_wait(ready.at[0], len(two_away))
+        for x in far_first(size_x):
+            signal(ready.at[1], device_b((x, 0), lead))
+
+
+    def scatter_arrived(place, carry):
+        other = partner(place)
+
+        @pl.when((place > 0) | jnp.logical_not(leads))
+        def _():
             cot_blocks(1, other).wait_recv()
-        if arrived:
-            spread[...] += scatter(arrived)
+
+        spread[...] += scatter(other)
+        return carry
+
+    lax.fori_loop(0, slabs, scatter_arrived, 0)
 
     later = [jnp.zeros((ROWS, WIDE), F32) for _ in range(3)]
     tail = jnp.zeros((ROWS, WIDE), F32)

time: 40.8 us -> 37.8 us (0.926)
  Pallas kernels: 40 us -> 37 us
    pallas_call x1, Pallas kernels: 38.7 us -> 35.7 us  [per_device(): pl.pallas_call(functools.partial(gradient_kernel, sizes, STEP_SPAN / tota...]
where the time goes in v6:
time: 37.8 us; the launch traced here: 37.7 us
  Pallas kernels  37 us (98%)
  between operations  0.64 us (2%)
    pallas_call x1, Pallas kernels, per_device(): pl.pallas_call(functools.partial(gradient_kernel, sizes, STEP_SPAN / tota...  35.7 us
    pallas_call x1, Pallas kernels, per_device(): pl.pallas_call(functools.partial(update_kernel, limit), out_shape=[jax.Sh...  1.33 us

profile of v6, /device:TPU:1, one launch (start us, length us, event | category | flops | bytes accessed | tf_op | source)
XLA Modules:
  0.0 37.7 jit_solution(7565700187384797769)
XLA Ops:
  0.6 35.7 %render_gradient.1 = (f32[4,16,8,256]{3,2,1,0:T(8,128)S(1)}, f32[4,16,8,256]{3,2,1,0:T(8,128)S(1)}, f32[4,16,8,256]{3,2,1,0:T(8,128)S(1)}, f32[4,16,8,256]{3,2,1,0:T(8,128)S(1)}, f32[1,128]{1,0:T(1,128)S(1)}) custom-call(f32[4,16,8,256]{3,2,1,0:T(8,128)} %grid_hbm.1, f32[4,16,8,256]{3,2,1,0:T(8,128)} %first_hbm.1, f32[4,16,8,256]{3,2,1,0:T(8,128)} %second_hbm.1, ...), custom_call_target="tpu_custom_call" | custom-call | tf_op jit(solution)/shard_map/render_gradient/pallas_call | solution.py:531
  36.3 1.3 %clipped_adam.1 = (f32[4,16,8,256]{3,2,1,0:T(8,128)}, f32[4,16,8,256]{3,2,1,0:T(8,128)}, f32[4,16,8,256]{3,2,1,0:T(8,128)}) custom-call(f32[4,16,8,256]{3,2,1,0:T(8,128)S(1)} %get-tuple-element.8.grid, f32[4,16,8,256]{3,2,1,0:T(8,128)S(1)} %get-tuple-element.9.first, f32[4,16,8,256]{3,2,1,0:T(8,128)S(1)} %get-tuple-element.10.second, ...), custom_call_target="tpu_custom_call" | custom-call | tf_op jit(solution)/shard_map/clipped_adam/pallas_call | solution.py:584

commit v7 on v6

--- a/solution.py
+++ b/solution.py
@@ -508,8 +508,12 @@
             held[0][c, z] = grid[c, z] - (rate * new_first) * pl.reciprocal(root + EPSILON)
             held[1][c, z] = new_first
             held[2][c, z] = new_second
-        for k in range(3):
-            pltpu.make_async_copy(held[k].at[c], outs[k].at[c], sem.at[k]).start()
+            if z % 4 == 3:
+                for k in range(3):
+                    part = (c, pl.ds(z - 3, 4))
+                    pltpu.make_async_copy(
+                        held[k].at[part], outs[k].at[part], sem.at[k]
+                    ).start()
     for k in range(3):
         pltpu.make_async_copy(held[k], outs[k], sem.at[k]).wait()
 

time: 37.8 us -> 37.7 us (level)
  no operation moved by 1% of the time
where the time goes in v7:
time: 37.7 us; the launch traced here: 37.6 us
  Pallas kernels  37 us (98%)
  between operations  0.64 us (2%)
    pallas_call x1, Pallas kernels, per_device(): pl.pallas_call(functools.partial(gradient_kernel, sizes, STEP_SPAN / tota...  35.7 us
    pallas_call x1, Pallas kernels, per_device(): pl.pallas_call(functools.partial(update_kernel, limit), out_shape=[jax.Sh...  1.26 us

profile of v7, /device:TPU:1, one launch (start us, length us, event | category | flops | bytes accessed | tf_op | source)
XLA Modules:
  0.0 37.6 jit_solution(3461065340004634882)
XLA Ops:
  0.6 35.7 %render_gradient.1 = (f32[4,16,8,256]{3,2,1,0:T(8,128)S(1)}, f32[4,16,8,256]{3,2,1,0:T(8,128)S(1)}, f32[4,16,8,256]{3,2,1,0:T(8,128)S(1)}, f32[4,16,8,256]{3,2,1,0:T(8,128)S(1)}, f32[1,128]{1,0:T(1,128)S(1)}) custom-call(f32[4,16,8,256]{3,2,1,0:T(8,128)} %grid_hbm.1, f32[4,16,8,256]{3,2,1,0:T(8,128)} %first_hbm.1, f32[4,16,8,256]{3,2,1,0:T(8,128)} %second_hbm.1, ...), custom_call_target="tpu_custom_call" | custom-call | tf_op jit(solution)/shard_map/render_gradient/pallas_call | solution.py:535
  36.3 1.3 %clipped_adam.1 = (f32[4,16,8,256]{3,2,1,0:T(8,128)}, f32[4,16,8,256]{3,2,1,0:T(8,128)}, f32[4,16,8,256]{3,2,1,0:T(8,128)}) custom-call(f32[4,16,8,256]{3,2,1,0:T(8,128)S(1)} %get-tuple-element.8.grid, f32[4,16,8,256]{3,2,1,0:T(8,128)S(1)} %get-tuple-element.9.first, f32[4,16,8,256]{3,2,1,0:T(8,128)S(1)} %get-tuple-element.10.second, ...), custom_call_target="tpu_custom_call" | custom-call | tf_op jit(solution)/shard_map/clipped_adam/pallas_call | solution.py:588
